TPU v7x, 32 devices: a whole 2x2x4 slice. The times are simulated.
32 devices in a mesh: tensor: 4 (over y, core), expert: 4 (over z), dp: 2 (over x).
Axes of the slice: x: 2, y: 2, z: 4, core: 2. Of those that a mesh axis runs over, the one named last changes fastest.
Arguments:
- grad_out: bfloat16 [512, 4096], P(('expert', 'dp')), may hold values from -6 to 6
- route_ids: int32 [512, 8], P(('expert', 'dp')), may hold values from 0 to 127, all different within a row; in each aligned block of 64 rows (0 to 63, 64 to 127, ...) at most 6 rows name the same one
- route_probs: bfloat16 [512, 8], P(('expert', 'dp')), may hold values from 0.019897461 to 0.5
- gate_act: bfloat16 [2, 128, 24, 768], P('dp', 'expert', None, 'tensor'), may hold values from -8 to 8
- up_act: bfloat16 [2, 128, 24, 768], P('dp', 'expert', None, 'tensor'), may hold values from -6 to 6
- w_down: bfloat16 [128, 768, 4096], P('expert', 'tensor'), may hold values from -0.21875 to 0.21875
Outputs:
- grad_gate: bfloat16 [2, 128, 24, 768], P('dp', 'expert', None, 'tensor')
- grad_up: bfloat16 [2, 128, 24, 768], P('dp', 'expert', None, 'tensor')
- grad_w_down: bfloat16 [128, 768, 4096], P('expert', 'tensor', 'dp')
- grad_probs: float32 [512, 8], P(('expert', 'dp'))
Inputs may be any that keep to these rules, and one draw needn't show every extreme that they name: `route_ids`: each row names 8 different experts. Within the 64 rows of one index pair of expert and dp no expert is named more than 6 times, and in every draw some expert is named exactly 6 times there.
All inputs are finite; a program needn't handle non-finite values.
Results may differ from a plain program's by a relative error of at most 0.009.
Values may be sent and summed in bfloat16 or wider, within the bound.
A program may use at most 192 MiB of HBM per device.

v0:
```python
import functools
import jax
import jax.numpy as jnp
from jax import lax
from jax.experimental import pallas as pl
from jax.experimental.pallas import tpu as pltpu
from jax.sharding import PartitionSpec as P


def on_device_wide(grad_out, route_ids, route_probs, gate_act, up_act, w_down):
    tok_count = grad_out.shape[0]
    top_count = route_ids.shape[1]
    expert_count = lax.axis_size("expert")
    tensor_count = lax.axis_size("tensor")
    local_experts = w_down.shape[0]
    experts = local_experts * expert_count
    slot_count = gate_act.shape[2]
    capacity = slot_count // expert_count
    model_width = grad_out.shape[1]
    quarter = model_width // tensor_count
    route_flat = route_ids.reshape(-1)
    expert_iota = lax.broadcasted_iota(jnp.int32, (1, experts), 1)
    matches = (route_flat[:, None] == expert_iota).astype(jnp.int32)
    earlier = jnp.cumsum(matches, axis=0) - matches
    position = jnp.sum(earlier * matches, axis=1)
    target = route_flat * capacity + position
    cell_iota = lax.broadcasted_iota(jnp.int32, (1, experts * capacity), 1)
    chosen = target[:, None] == cell_iota
    chosen_weight = chosen.astype(jnp.float32)
    token_chosen = jnp.sum(
        chosen_weight.reshape(tok_count, top_count, experts * capacity), axis=1
    ).astype(jnp.bfloat16)
    own_columns = lax.dynamic_slice_in_dim(grad_out, lax.axis_index("tensor") * quarter, quarter, 1)
    send_rows = jnp.einsum(
        "nf,nd->fd", token_chosen, own_columns, preferred_element_type=jnp.float32
    ).astype(jnp.bfloat16)
    send_probs = jnp.sum(
        chosen_weight * route_probs.reshape(-1).astype(jnp.float32)[:, None], axis=0
    ).astype(jnp.bfloat16)
    send_rows = send_rows.reshape(expert_count, local_experts, capacity, quarter)
    send_probs = send_probs.reshape(expert_count, local_experts, capacity)
    arrived_rows, arrived_probs = (
        lax.all_to_all(send_rows, "expert", split_axis=0, concat_axis=0, tiled=True),
        lax.all_to_all(send_probs, "expert", split_axis=0, concat_axis=0, tiled=True),
    )
    gathered = lax.all_gather(arrived_rows, "tensor", axis=3, tiled=True)
    slot_rows = jnp.transpose(gathered, (1, 0, 2, 3)).reshape(
        local_experts, slot_count, model_width
    )
    slot_probs = (
        jnp.transpose(arrived_probs, (1, 0, 2))
        .reshape(local_experts, slot_count)
        .astype(jnp.float32)
    )
    gate_pre = gate_act[0].astype(jnp.float32)
    up_pre = up_act[0].astype(jnp.float32)
    grad_hidden = jnp.einsum("jsd,jfd->jsf", slot_rows, w_down, preferred_element_type=jnp.float32)
    sigmoid_gate = jax.nn.sigmoid(gate_pre)
    silu_gate = gate_pre * sigmoid_gate
    hidden = (silu_gate * up_pre).astype(jnp.bfloat16)
    partial_dot = jnp.sum(grad_hidden * hidden.astype(jnp.float32), axis=2)
    grad_scaled = slot_probs[:, :, None] * grad_hidden
    grad_up = (grad_scaled * silu_gate).astype(jnp.bfloat16)
    grad_gate = (
        grad_scaled * up_pre * sigmoid_gate * (1.0 + gate_pre * (1.0 - sigmoid_gate))
    ).astype(jnp.bfloat16)
    scaled_rows = (slot_probs[:, :, None] * slot_rows.astype(jnp.float32)).astype(jnp.bfloat16)
    replica_count = lax.axis_size("dp")
    column_count = model_width // replica_count
    split_rows = jnp.transpose(
        scaled_rows.reshape(local_experts, slot_count, replica_count, column_count), (2, 0, 1, 3)
    )
    columns = lax.all_to_all(split_rows, "dp", split_axis=0, concat_axis=0, tiled=True)
    initial = jnp.zeros((local_experts, hidden.shape[2], column_count), jnp.float32)
    hidden_block = lax.all_gather(hidden[None], "dp", axis=0, tiled=True)

    def add_member(member, summed):
        hid_one = lax.dynamic_index_in_dim(hidden_block, member, 0, keepdims=False)
        col_one = lax.dynamic_index_in_dim(columns, member, 0, keepdims=False)
        term = jnp.einsum("jsf,jsd->jfd", hid_one, col_one, preferred_element_type=jnp.float32)
        rounded = lax.optimization_barrier(term.astype(jnp.bfloat16))
        return summed + rounded.astype(jnp.float32)

    grad_weight = lax.fori_loop(0, hidden_block.shape[0], add_member, initial).astype(jnp.bfloat16)
    prob_cells = jnp.transpose(
        partial_dot.reshape(local_experts, expert_count, capacity), (1, 0, 2)
    )
    prob_cells = lax.psum(prob_cells, "tensor")
    returned = lax.all_to_all(prob_cells, "expert", split_axis=0, concat_axis=0, tiled=True)
    returned_flat = returned.reshape(-1)
    grad_probs = jnp.sum(jnp.where(chosen, returned_flat[None, :], 0.0), axis=1).reshape(
        tok_count, top_count
    )
    return (grad_gate[None], grad_up[None], grad_weight, grad_probs)


MESH = pl.DeviceIdType.MESH


def collect_kernel(sizes, x_ref, meta_ref, hid_ref, tok, oth, metas, hid_oth, local, zs, zr, ms, mr, hs, hr, xs, xr, ys, yr, vs, vr, cs, cr):
    tn, en, rn = sizes
    t, e, d = lax.axis_index("tensor"), lax.axis_index("expert"), lax.axis_index("dp")
    across = lax.rem(t + 2, tn)
    mate = t + 1 - 2 * lax.rem(t, 2)
    far = 1 - d
    barrier = pltpu.get_barrier_semaphore()
    others = []
    for i in range(en):
        for j in range(rn):
            if i or j:
                others.append((t, lax.rem(e + i, en), lax.rem(d + j, rn)))
    peers = others + [(across, e, d), (mate, e, d)]
    for peer in peers:
        pl.semaphore_signal(barrier, inc=1, device_id=peer, device_id_type=MESH)
    pl.semaphore_wait(barrier, len(peers))

    def send(src, dst, ssem, rsem, peer):
        copy = pltpu.make_async_remote_copy(
            src_ref=src, dst_ref=dst, send_sem=ssem, recv_sem=rsem, device_id=peer, device_id_type=MESH
        )
        copy.start()
        return copy

    mine = [
        pltpu.make_async_copy(x_ref, tok.at[t, e], local.at[0]),
        pltpu.make_async_copy(meta_ref, metas.at[e, d], local.at[1]),
    ]
    for copy in mine:
        copy.start()
    z = [
        send(x_ref, tok.at[t, e], zs.at[j - 1], zr.at[j - 1], (t, lax.rem(e + j, en), d))
        for j in range(1, en)
    ]
    m = [send(meta_ref, metas.at[e, d], ms.at[i], mr.at[i], peer) for i, peer in enumerate(others)]
    y = [send(x_ref, tok.at[t, e], ys.at[0], yr.at[0], (across, e, d))]
    x = [send(x_ref.at[far], oth.at[t, e], xs.at[0], xr.at[0], (t, e, far))]
    for j in range(1, en):
        z[j - 1].wait_recv()
        b = lax.rem(e - j + en, en)
        x.append(send(tok.at[t, b, far], oth.at[t, b], xs.at[j], xr.at[j], (t, e, far)))
        y.append(send(tok.at[t, b], tok.at[t, b], ys.at[j], yr.at[j], (across, e, d)))
    h = send(hid_ref, hid_oth, hs, hr, (t, e, far))
    v = []
    for j in range(en):
        x[j].wait_recv()
        b = lax.rem(e - j + en, en)
        v.append(send(oth.at[t, b], oth.at[t, b], vs.at[j], vr.at[j], (across, e, d)))
    for copy in mine:
        copy.wait()
    c = [
        send(tok.at[t], tok.at[t], cs.at[0], cr.at[0], (mate, e, d)),
        send(oth.at[t], oth.at[t], cs.at[1], cr.at[1], (mate, e, d)),
    ]
    for copy in y:
        copy.wait_recv()
    c.append(send(tok.at[across], tok.at[across], cs.at[2], cr.at[2], (mate, e, d)))
    for copy in v:
        copy.wait_recv()
    c.append(send(oth.at[across], oth.at[across], cs.at[3], cr.at[3], (mate, e, d)))
    for copy in m + c + [h]:
        copy.wait_recv()
    for copy in z + m + y + x + v + c + [h]:
        copy.wait_send()


def return_kernel(sizes, x_ref, out, local, ss, rs):
    tn, en = sizes
    t, e, d = lax.axis_index("tensor"), lax.axis_index("expert"), lax.axis_index("dp")
    barrier = pltpu.get_barrier_semaphore()
    peers = []
    for i in range(tn):
        for j in range(en):
            if i or j:
                peers.append((lax.rem(t + i, tn), lax.rem(e + j, en), d))
    for peer in peers:
        pl.semaphore_signal(barrier, inc=1, device_id=peer, device_id_type=MESH)
    pl.semaphore_wait(barrier, len(peers))
    mine = pltpu.make_async_copy(x_ref.at[e], out.at[t, e], local)
    mine.start()
    copies = []
    for i, peer in enumerate(peers):
        copy = pltpu.make_async_remote_copy(
            src_ref=x_ref.at[peer[1]], dst_ref=out.at[t, e], send_sem=ss.at[i], recv_sem=rs.at[i],
            device_id=peer, device_id_type=MESH,
        )
        copy.start()
        copies.append(copy)
    mine.wait()
    for copy in copies:
        copy.wait()


def expert_kernel(rows, scaled, hid_own, hid_far, gate, up, prob, w, grad_gate, grad_up, grad_w, dot):
    slots = rows.shape[1]
    turned = lax.dot_general(
        w[0], rows[0], (((1,), (1,)), ((), ())), preferred_element_type=jnp.float32
    )
    grad_hidden = turned.T
    g = gate[0, 0].astype(jnp.float32)
    u = up[0, 0].astype(jnp.float32)
    s = jax.nn.sigmoid(g)
    silu = g * s
    hidden = hid_own[0]
    dot[0] = jnp.sum(grad_hidden * hidden.astype(jnp.float32), axis=1, keepdims=True)
    weighted = prob[0] * grad_hidden
    grad_up[0, 0] = (weighted * silu).astype(jnp.bfloat16)
    grad_gate[0, 0] = (weighted * u * s * (1.0 + g * (1.0 - s))).astype(jnp.bfloat16)
    both = jnp.concatenate([hidden.astype(jnp.float32), hid_far[0].astype(jnp.float32)], axis=0)
    both = both.T.astype(jnp.bfloat16)
    grad_w[0] = jnp.dot(both, scaled[0], preferred_element_type=jnp.float32).astype(jnp.bfloat16)


def on_device(grad_out, route_ids, route_probs, gate_act, up_act, w_down):
    tokens, width = grad_out.shape
    top = route_ids.shape[1]
    tn, en, rn = lax.axis_size("tensor"), lax.axis_size("expert"), lax.axis_size("dp")
    t, e, d = lax.axis_index("tensor"), lax.axis_index("expert"), lax.axis_index("dp")
    local, units, slots = w_down.shape[0], w_down.shape[1], gate_act.shape[2]
    cap = slots // en
    strip = width // (tn * rn)
    half = width // rn
    f32, bf16 = jnp.float32, jnp.bfloat16
    sem = pltpu.SemaphoreType.DMA
    vmem = pl.BlockSpec(memory_space=pltpu.VMEM)
    g = gate_act[0].astype(f32)
    hidden = (g * jax.nn.sigmoid(g) * up_act[0].astype(f32)).astype(bf16)
    parts = jnp.transpose(grad_out.reshape(tokens, rn, tn, strip), (2, 1, 0, 3))
    mine = lax.dynamic_index_in_dim(parts, t, 0, keepdims=False)
    meta = jnp.concatenate([route_ids.T.astype(f32), route_probs.T.astype(f32)], axis=1)
    tok, oth, metas, hid_far = pl.pallas_call(
        functools.partial(collect_kernel, (tn, en, rn)),
        out_shape=(
            jax.ShapeDtypeStruct((tn, en, rn, tokens, strip), bf16),
            jax.ShapeDtypeStruct((tn, en, tokens, strip), bf16),
            jax.ShapeDtypeStruct((en, rn) + meta.shape, f32),
            jax.ShapeDtypeStruct(hidden.shape, bf16),
        ),
        in_specs=[vmem] * 3,
        out_specs=(vmem,) * 4,
        scratch_shapes=[
            sem((2,)), sem((en - 1,)), sem((en - 1,)), sem((en * rn - 1,)), sem((en * rn - 1,)), sem, sem,
            sem((en,)), sem((en,)), sem((en,)), sem((en,)), sem((en,)), sem((en,)), sem((4,)), sem((4,)),
        ],
        compiler_params=pltpu.CompilerParams(collective_id=0, has_side_effects=True),
    )(mine, meta, hidden)

    ids = metas[..., :tokens].astype(jnp.int32)
    probs = metas[..., tokens:]
    here = e * local + jnp.arange(local, dtype=jnp.int32)
    hit = ids[:, :, :, None, :] == here[:, None]
    named = jnp.any(hit, axis=2)
    weight = jnp.sum(jnp.where(hit, probs[:, :, :, None, :], 0.0), axis=2)
    below = jnp.arange(tokens)[:, None] < jnp.arange(tokens)[None, :]
    position = jnp.einsum("erxn,nm->erxm", named.astype(bf16), below.astype(bf16), preferred_element_type=f32)
    place = jnp.where(named, position, -1.0)
    spots = place[:, :, :, None, :] == jnp.arange(cap, dtype=f32)[:, None]
    spots = jnp.transpose(spots, (1, 2, 0, 3, 4))
    carried = jnp.transpose(weight, (1, 2, 0, 3))[:, :, :, None, :]
    same = (jnp.arange(en)[:, None] == jnp.arange(en)[None, :])[None, None, :, None, :, None]
    one = (spots[:, :, :, :, None, :] & same).reshape(rn, local * slots, en * tokens)
    wide = jnp.where(spots, carried, 0.0)
    slot_probs = lax.dynamic_index_in_dim(jnp.sum(wide, axis=-1), d, 0, keepdims=False).reshape(local, slots, 1)
    wide = jnp.where(same, wide[:, :, :, :, None, :], 0.0).astype(bf16).reshape(rn, local * slots, en * tokens)
    pick = lambda a, i: lax.dynamic_index_in_dim(a, i, 0, keepdims=False)
    flat = jnp.transpose(tok, (1, 3, 2, 0, 4)).reshape(en * tokens, width)
    far_flat = jnp.transpose(oth, (1, 2, 0, 3)).reshape(en * tokens, half)
    near_flat = lax.dynamic_slice_in_dim(flat, d * half, half, 1)
    rows = jnp.dot(pick(one, d).astype(bf16), flat, preferred_element_type=f32).astype(bf16).reshape(local, slots, width)
    near = jnp.dot(pick(wide, d), near_flat, preferred_element_type=f32).astype(bf16).reshape(local, slots, half)
    far = jnp.dot(pick(wide, 1 - d), far_flat, preferred_element_type=f32).astype(bf16).reshape(local, slots, half)
    scaled = jnp.concatenate([near, far], axis=1)

    def block(*shape):
        return pl.BlockSpec((1,) + shape, lambda i: (i,) + (0,) * len(shape))

    act = pl.BlockSpec((1, 1, slots, units), lambda i: (0, i, 0, 0))
    act_shape = jax.ShapeDtypeStruct((1, local, slots, units), bf16)
    grad_gate, grad_up, grad_w, dot = pl.pallas_call(
        expert_kernel,
        grid=(local,),
        in_specs=[
            block(slots, width), block(2 * slots, half), block(slots, units), block(slots, units), act, act,
            block(slots, 1), block(units, width),
        ],
        out_specs=(act, act, block(units, half), block(slots, 1)),
        out_shape=(
            act_shape, act_shape,
            jax.ShapeDtypeStruct((local, units, half), bf16),
            jax.ShapeDtypeStruct((local, slots, 1), f32),
        ),
    )(rows, scaled, hidden, hid_far, gate_act, up_act, slot_probs, w_down)

    cells = jnp.transpose(dot.reshape(local, en, cap), (1, 0, 2)).reshape(en, local * cap)
    room = -(-local * cap // 1024) * 1024
    cells = jnp.pad(cells, ((0, 0), (0, room - local * cap))).reshape(en, room // 128, 128)
    back = pl.pallas_call(
        functools.partial(return_kernel, (tn, en)),
        out_shape=jax.ShapeDtypeStruct((tn,) + cells.shape, f32),
        in_specs=[vmem],
        out_specs=vmem,
        scratch_shapes=[sem, sem((tn * en - 1,)), sem((tn * en - 1,))],
        compiler_params=pltpu.CompilerParams(collective_id=1, has_side_effects=True),
    )(cells)
    back = jnp.sum(back, axis=0).reshape(en, room)[:, : local * cap].reshape(1, 1, -1)
    every = jnp.arange(en * local, dtype=jnp.int32)
    match = route_ids[:, :, None] == every
    count = jnp.any(match, axis=1)
    before = jnp.einsum("nx,nm->mx", count.astype(bf16), below.astype(bf16), preferred_element_type=f32)
    at = jnp.sum(jnp.where(match, before[:, None, :], 0.0), axis=2).astype(jnp.int32)
    target = route_ids * cap + at
    chosen = target[:, :, None] == jnp.arange(en * local * cap, dtype=jnp.int32)
    grad_probs = jnp.sum(jnp.where(chosen, back, 0.0), axis=2)
    return grad_gate, grad_up, grad_w, grad_probs


def solution(mesh):
    sizes = mesh.shape
    small = sizes["tensor"] == 4 and sizes["dp"] == 2 and sizes["expert"] <= 8
    placed = (
        P(("expert", "dp"), None),
        P(("expert", "dp"), None),
        P(("expert", "dp"), None),
        P("dp", "expert", None, "tensor"),
        P("dp", "expert", None, "tensor"),
        P("expert", "tensor", None),
    )
    return jax.shard_map(
        on_device if small else on_device_wide,
        mesh=mesh,
        in_specs=placed,
        out_specs=(
            P("dp", "expert", None, "tensor"),
            P("dp", "expert", None, "tensor"),
            P("expert", "tensor", "dp"),
            P(("expert", "dp"), None),
        ),
        check_vma=False,
    )
```

profile of v0, /device:TPU:0, one launch (start us, length us, event | category | flops | bytes accessed | tf_op | source)
XLA Modules:
  0.0 138.3 jit_solution(426419056676716856)
XLA Ops:
  0.6 1.4 %reshape.87 = bf16[64,2,4,512]{3,2,1,0:T(4,128)(2,1)S(1)} reshape(bf16[64,4096]{1,0:T(8,128)(2,1)} %param.6) | data formatting | bytes 1048576 | tf_op jit(solution)/shard_map/reshape | solution.py:227
  2.1 0.3 constant_dynamic-slice_fusion.1
  2.4 0.7 copy.69
  3.1 0.8 copy.45
  4.5 0.8 convert_add_fusion
  5.3 0.7 convert_bitcast_fusion
  6.0 0.7 pad_maximum_fusion.1.meta_ref
  6.6 2.1 %fusion.7.hid_ref.hid_own = bf16[32,24,192]{2,1,0:T(8,128)(2,1)} fusion(bf16[1,32,24,192]{3,2,1,0:T(8,128)(2,1)} %up.1, bf16[1,32,24,192]{3,2,1,0:T(8,128)(2,1)} %gate.1), kind=kLoop, calls=%fused_computation.20 | loop fusion | flops 1179648 | bytes 884736 | tf_op jit(solution)/shard_map/convert_element_type | solution.py:226
  8.8 34.0 %shard_map.93 = (bf16[4,4,2,64,512]{4,3,2,1,0:T(8,128)(2,1)}, bf16[4,4,64,512]{3,2,1,0:T(8,128)(2,1)}, f32[4,2,8,128]{3,2,1,0:T(8,128)}, bf16[32,24,192]{2,1,0:T(8,128)(2,1)}) custom-call(bf16[2,64,512]{2,1,0:T(8,128)(2,1)} %bitcast.71, f32[8,128]{1,0:T(8,128)} %pad_maximum_fusion.1.meta_ref, bf16[32,24,192]{2,1,0:T(8,128)(2,1)} %fusion.7.hid_ref.hid_own), custom_call_target="tpu_custom_call" | custom-call | tf_op jit(solution)/shard_map/pallas_call | solution.py:230
  42.7 0.9 fusion.23
  44.7 0.5 broadcast_in_dim.95
  45.3 1.0 broadcast_in_dim.96
  46.5 0.6 and.32
  47.1 1.1 select_convert_fusion
  48.2 3.2 %copy.40 = bf16[4,64,2,4,512]{4,3,2,1,0:T(4,128)(2,1)S(1)} copy(bf16[4,64,2,4,512]{4,1,2,0,3:T(8,128)(2,1)} %bitcast.69) | data formatting | bytes 4194304 | tf_op jit(solution)/shard_map/transpose | solution.py:265
  51.4 2.8 %reshape.88 = bf16[256,4096]{1,0:T(8,128)(2,1)} reshape(bf16[4,64,2,4,512]{4,3,2,1,0:T(4,128)(2,1)S(1)} %copy.40) | data formatting | bytes 4194304 | tf_op jit(solution)/shard_map/reshape | solution.py:265
  54.2 2.3 %convolution_convert_fusion.2 = bf16[768,2048]{1,0:T(8,128)(2,1)S(1)} fusion(bf16[256,4096]{1,0:T(8,128)(2,1)} %reshape.88, s32[]{:T(128)S(6)} %select_n.58, bf16[2,768,256]{2,1,0:T(8,128)(2,1)} %select_convert_fusion, s32[]{:T(128)S(6)} %select_n.54), kind=kOutput, calls=%fused_computation.3 | convolution fusion | flops 806879232 | bytes 4587528 | tf_op jit(solution)/shard_map/dot_general | solution.py:269
  56.5 2.1 %copy.43 = bf16[4,64,4,512]{3,2,1,0:T(4,128)(2,1)S(1)} copy(bf16[4,64,4,512]{3,1,0,2:T(8,128)(2,1)} %bitcast.70) | data formatting | bytes 2097152 | tf_op jit(solution)/shard_map/transpose | solution.py:266
  58.9 1.0 convolution_convert_fusion.1
  59.9 3.6 %pad_maximum_fusion.scaled = bf16[32,48,2048]{2,1,0:T(8,128)(2,1)} fusion(bf16[32,24,2048]{2,1,0:T(8,128)(2,1)S(1)} %bitcast.65, bf16[32,24,2048]{2,1,0:T(8,128)(2,1)S(1)} %bitcast.66), kind=kLoop, calls=%fused_computation.1 | loop fusion | flops 12582912 | bytes 12582912 | tf_op jit(solution)/shard_map/concatenate | solution.py:271
  63.6 0.3 fusion.16
  63.9 1.0 copy.44.prob
  65.1 0.8 and.29
  65.9 2.1 %and.30 = pred[2,768,256]{2,1,0:T(32,128)(4,1)} reshape(pred[2,32,4,6,4,64]{5,4,3,2,1,0:T(4,128)(4,1)S(1)} %and.29) | data formatting | bytes 786432 | tf_op jit(solution)/shard_map/and | solution.py:260
  68.0 5.4 %convolution_convert_fusion = bf16[768,4096]{1,0:T(8,128)(2,1)} fusion(bf16[256,4096]{1,0:T(8,128)(2,1)S(1)} %copy-done, pred[2,768,256]{2,1,0:T(32,128)(4,1)} %and.30, s32[]{:T(128)S(6)} %select_n.54, pred[768,256]{1,0:T(8,128)(4,1)S(1)} %and.32), kind=kOutput, calls=%fused_computation | convolution fusion | flops 1613955072 | bytes 8781828 | tf_op jit(solution)/shard_map/dot_general | solution.py:268
  73.4 51.3 %shard_map.94 = (bf16[1,32,24,192]{3,2,1,0:T(8,128)(2,1)}, bf16[1,32,24,192]{3,2,1,0:T(8,128)(2,1)}, bf16[32,192,2048]{2,1,0:T(8,128)(2,1)}, f32[32,24,1]{2,1,0:T(8,128)}) custom-call(bf16[32,24,4096]{2,1,0:T(8,128)(2,1)} %bitcast.64, bf16[32,48,2048]{2,1,0:T(8,128)(2,1)} %pad_maximum_fusion.scaled, bf16[32,24,192]{2,1,0:T(8,128)(2,1)} %fusion.7.hid_ref.hid_own, ...), custom_call_target="tpu_custom_call" | custom-call | tf_op jit(solution)/shard_map/pallas_call | solution.py:278
  124.7 1.2 copy.48
  126.1 0.6 copy.71
  126.7 9.6 %shard_map.95 = f32[4,4,8,128]{3,2,1,0:T(8,128)} custom-call(f32[4,8,128]{2,1,0:T(8,128)} %bitcast.74), custom_call_target="tpu_custom_call" | custom-call | tf_op jit(solution)/shard_map/pallas_call | solution.py:296
  136.3 0.9 reduce_sum.48
  137.4 0.3 select_reduce_fusion
  137.7 0.7 copy.50
  (33 shorter events, 2.9 us)
Async XLA Ops:
  43.9 0.7 copy-start.2
  56.5 2.4 %copy-start.1 = (bf16[2,768,256]{2,1,0:T(8,128)(2,1)S(1)}, bf16[2,768,256]{2,1,0:T(8,128)(2,1)}, u32[]{:S(2)}) copy-start(bf16[2,768,256]{2,1,0:T(8,128)(2,1)} %select_convert_fusion) | copy-start | bytes 2359300
  59.9 3.6 %copy-start.3 = (f32[4,2,32,64]{3,2,1,0:T(8,128)S(1)}, f32[4,2,32,64]{3,2,1,0:T(8,128)}, u32[]{:S(2)}) copy-start(f32[4,2,32,64]{3,2,1,0:T(8,128)} %copy-done.2) | copy-start | bytes 196612
  63.6 4.4 %copy-start = (bf16[256,4096]{1,0:T(8,128)(2,1)S(1)}, bf16[256,4096]{1,0:T(8,128)(2,1)}, u32[]{:S(2)}) copy-start(bf16[256,4096]{1,0:T(8,128)(2,1)} %reshape.88) | copy-start | bytes 6291460
where the time goes:
time: 139 us; the launch traced here: 138 us
  Pallas kernels  94.9 us (68%)
  local copies, waits for them, and re-layouts  21.2 us (15%)
  other arithmetic  12.3 us (9%)
  matrix products  9.07 us (7%)
    pallas_call x1, Pallas kernels, on_device(): pl.pallas_call(expert_kernel, grid=(local,), in_specs=[block(slots, width...  51.3 us
    pallas_call x1, Pallas kernels, on_device(): pl.pallas_call(functools.partial(collect_kernel, (tn, en, rn)), out_shape...  34 us
    pallas_call x1, Pallas kernels, on_device(): pl.pallas_call(functools.partial(return_kernel, (tn, en)), out_shape=jax....  9.61 us
    dot_general x1, matrix products, on_device(): jnp.dot(pick(one, d).astype(bf16), flat, preferred_element_type=f32)  5.38 us
    and x4, local copies, waits for them, and re-layouts, on_device(): spots[:, :, :, :, None, :] & same  3.68 us
    concatenate x1, other arithmetic, on_device(): scaled = jnp.concatenate([near, far], axis=1)  3.62 us
    unnamed x15, local copies, waits for them, and re-layouts  3.21 us
    transpose x1, local copies, waits for them, and re-layouts, on_device(): flat = jnp.transpose(tok, (1, 3, 2, 0, 4)).reshape(en * tokens, width)  3.21 us

commit v1 on v0

v1 whole, which is shorter than its diff:
```python
import functools
import jax
import jax.numpy as jnp
from jax import lax
from jax.experimental import pallas as pl
from jax.experimental.pallas import tpu as pltpu
from jax.sharding import PartitionSpec as P


def on_device_wide(grad_out, route_ids, route_probs, gate_act, up_act, w_down):
    tok_count = grad_out.shape[0]
    top_count = route_ids.shape[1]
    expert_count = lax.axis_size("expert")
    tensor_count = lax.axis_size("tensor")
    local_experts = w_down.shape[0]
    experts = local_experts * expert_count
    slot_count = gate_act.shape[2]
    capacity = slot_count // expert_count
    model_width = grad_out.shape[1]
    quarter = model_width // tensor_count
    route_flat = route_ids.reshape(-1)
    expert_iota = lax.broadcasted_iota(jnp.int32, (1, experts), 1)
    matches = (route_flat[:, None] == expert_iota).astype(jnp.int32)
    earlier = jnp.cumsum(matches, axis=0) - matches
    position = jnp.sum(earlier * matches, axis=1)
    target = route_flat * capacity + position
    cell_iota = lax.broadcasted_iota(jnp.int32, (1, experts * capacity), 1)
    chosen = target[:, None] == cell_iota
    chosen_weight = chosen.astype(jnp.float32)
    token_chosen = jnp.sum(
        chosen_weight.reshape(tok_count, top_count, experts * capacity), axis=1
    ).astype(jnp.bfloat16)
    own_columns = lax.dynamic_slice_in_dim(grad_out, lax.axis_index("tensor") * quarter, quarter, 1)
    send_rows = jnp.einsum(
        "nf,nd->fd", token_chosen, own_columns, preferred_element_type=jnp.float32
    ).astype(jnp.bfloat16)
    send_probs = jnp.sum(
        chosen_weight * route_probs.reshape(-1).astype(jnp.float32)[:, None], axis=0
    ).astype(jnp.bfloat16)
    send_rows = send_rows.reshape(expert_count, local_experts, capacity, quarter)
    send_probs = send_probs.reshape(expert_count, local_experts, capacity)
    arrived_rows, arrived_probs = (
        lax.all_to_all(send_rows, "expert", split_axis=0, concat_axis=0, tiled=True),
        lax.all_to_all(send_probs, "expert", split_axis=0, concat_axis=0, tiled=True),
    )
    gathered = lax.all_gather(arrived_rows, "tensor", axis=3, tiled=True)
    slot_rows = jnp.transpose(gathered, (1, 0, 2, 3)).reshape(
        local_experts, slot_count, model_width
    )
    slot_probs = (
        jnp.transpose(arrived_probs, (1, 0, 2))
        .reshape(local_experts, slot_count)
        .astype(jnp.float32)
    )
    gate_pre = gate_act[0].astype(jnp.float32)
    up_pre = up_act[0].astype(jnp.float32)
    grad_hidden = jnp.einsum("jsd,jfd->jsf", slot_rows, w_down, preferred_element_type=jnp.float32)
    sigmoid_gate = jax.nn.sigmoid(gate_pre)
    silu_gate = gate_pre * sigmoid_gate
    hidden = (silu_gate * up_pre).astype(jnp.bfloat16)
    partial_dot = jnp.sum(grad_hidden * hidden.astype(jnp.float32), axis=2)
    grad_scaled = slot_probs[:, :, None] * grad_hidden
    grad_up = (grad_scaled * silu_gate).astype(jnp.bfloat16)
    grad_gate = (
        grad_scaled * up_pre * sigmoid_gate * (1.0 + gate_pre * (1.0 - sigmoid_gate))
    ).astype(jnp.bfloat16)
    scaled_rows = (slot_probs[:, :, None] * slot_rows.astype(jnp.float32)).astype(jnp.bfloat16)
    replica_count = lax.axis_size("dp")
    column_count = model_width // replica_count
    split_rows = jnp.transpose(
        scaled_rows.reshape(local_experts, slot_count, replica_count, column_count), (2, 0, 1, 3)
    )
    columns = lax.all_to_all(split_rows, "dp", split_axis=0, concat_axis=0, tiled=True)
    initial = jnp.zeros((local_experts, hidden.shape[2], column_count), jnp.float32)
    hidden_block = lax.all_gather(hidden[None], "dp", axis=0, tiled=True)

    def add_member(member, summed):
        hid_one = lax.dynamic_index_in_dim(hidden_block, member, 0, keepdims=False)
        col_one = lax.dynamic_index_in_dim(columns, member, 0, keepdims=False)
        term = jnp.einsum("jsf,jsd->jfd", hid_one, col_one, preferred_element_type=jnp.float32)
        rounded = lax.optimization_barrier(term.astype(jnp.bfloat16))
        return summed + rounded.astype(jnp.float32)

    grad_weight = lax.fori_loop(0, hidden_block.shape[0], add_member, initial).astype(jnp.bfloat16)
    prob_cells = jnp.transpose(
        partial_dot.reshape(local_experts, expert_count, capacity), (1, 0, 2)
    )
    prob_cells = lax.psum(prob_cells, "tensor")
    returned = lax.all_to_all(prob_cells, "expert", split_axis=0, concat_axis=0, tiled=True)
    returned_flat = returned.reshape(-1)
    grad_probs = jnp.sum(jnp.where(chosen, returned_flat[None, :], 0.0), axis=1).reshape(
        tok_count, top_count
    )
    return (grad_gate[None], grad_up[None], grad_weight, grad_probs)


MESH = pl.DeviceIdType.MESH
RING = 6


def gather_kernel(
    sizes, cap, x_ref, ids_ref, probs_ref, gate_ref, up_ref, w_ref,
    rows_out, hs_out, gh_out, prob_out, back,
    tok, oth, ids, probs, gate, up, wbuf, rows, far_rows, one, acc, gh, hid, hs, hs_far, prob, cells,
    lx, lm, la, lw, lo, zs, zr, ms, mr, ys, yr, as_, ar, bs, br, xs, xr, ps, pr, qs, qr, us, ur, hsem, rs, rr,
):
    tn, en, rn = sizes
    f32, bf16 = jnp.float32, jnp.bfloat16
    t, e, d = lax.axis_index("tensor"), lax.axis_index("expert"), lax.axis_index("dp")
    plane, core = t // 2, lax.rem(t, 2)
    across = lax.rem(t + 2, tn)
    mate = t + 1 - 2 * core
    far = 1 - d
    steps = tok.shape[0] // 2
    per = steps // 2
    tokens, width = x_ref.shape
    region = tok.shape[2]
    piece = region // 2
    local, slots, units = gh.shape
    total = en * tokens

    def block(k):
        return lax.rem(e - k + en, en)

    def index(s, p):
        half = jnp.where(s < per, far, d)
        return half * steps + p * per + lax.rem(s, per)

    def part(buf, g, b, q):
        return buf.at[g, pl.ds(pl.multiple_of(b * tokens, tokens), tokens), pl.ds(pl.multiple_of(q * piece, piece), piece)]

    def wide_part(buf, g, q):
        return buf.at[g, :, pl.ds(pl.multiple_of(q * piece, piece), piece)]

    def remote(src, dst, ssem, rsem, peer):
        return pltpu.make_async_remote_copy(
            src_ref=src, dst_ref=dst, send_sem=ssem, recv_sem=rsem, device_id=peer, device_id_type=MESH
        )

    def along(s, k):
        ref = part(tok, index(s, plane), e, core)
        return remote(ref, ref, zs.at[s, k - 1], zr.at[s, k - 1], (t, lax.rem(e + k, en), d))

    def over(s, k):
        ref = part(tok, index(s, plane), block(k), core)
        return remote(ref, ref, ys.at[s, k - 1], yr.at[s, k - 1], (across, e, d))

    def mate_own(s, k):
        ref = part(tok, index(s, plane), block(k), core)
        return remote(ref, ref, as_.at[s, k - 1], ar.at[s, k - 1], (mate, e, d))

    def mate_over(s, k):
        ref = part(tok, index(s, 1 - plane), block(k), core)
        return remote(ref, ref, bs.at[s, k - 1], br.at[s, k - 1], (mate, e, d))

    def far_send(i):
        return remote(
            wide_part(tok, index(i, plane), core), wide_part(oth, plane * per + i, core), xs.at[i], xr.at[i], (t, e, far)
        )

    def far_over(i):
        ref = wide_part(oth, plane * per + i, core)
        return remote(ref, ref, ps.at[i], pr.at[i], (across, e, d))

    def far_mate(i):
        ref = wide_part(oth, plane * per + i, core)
        return remote(ref, ref, qs.at[i], qr.at[i], (mate, e, d))

    def far_mate_over(i):
        ref = wide_part(oth, (1 - plane) * per + i, core)
        return remote(ref, ref, us.at[i], ur.at[i], (mate, e, d))

    def hid_send():
        return remote(hs, hs_far, hsem.at[0], hsem.at[1], (t, e, far))

    def weights(r):
        g = index(r // 2, jnp.where(lax.rem(r, 2) == 0, plane, 1 - plane))
        slot = lax.rem(r, RING)
        return pltpu.make_async_copy(
            w_ref.at[:, :, pl.ds(pl.multiple_of(g * region, region), region)], wbuf.at[slot], lw.at[slot]
        )

    def load_own(g):
        return pltpu.make_async_copy(
            x_ref.at[:, pl.ds(g * region, region)],
            tok.at[g, pl.ds(pl.multiple_of(e * tokens, tokens), tokens), :], lx.at[g],
        )

    loads = [load_own(g) for g in range(2 * steps)]
    metas = [
        pltpu.make_async_copy(ids_ref, ids.at[e, d], lm.at[0]),
        pltpu.make_async_copy(probs_ref, probs.at[e, d], lm.at[1]),
    ]
    acts = [pltpu.make_async_copy(gate_ref.at[0], gate, la.at[0]), pltpu.make_async_copy(up_ref.at[0], up, la.at[1])]
    for copy in metas + loads + acts:
        copy.start()
    for r in range(RING):
        weights(r).start()

    others = []
    for i in range(en):
        for j in range(rn):
            if i or j:
                others.append((t, lax.rem(e + i, en), lax.rem(d + j, rn)))
    group = []
    for i in range(tn):
        for j in range(en):
            if i or j:
                group.append((lax.rem(t + i, tn), lax.rem(e + j, en), d))
    greet = group + [peer for n, peer in enumerate(others) if (n + 1) % rn]
    barrier = pltpu.get_barrier_semaphore()
    for peer in greet:
        pl.semaphore_signal(barrier, inc=1, device_id=peer, device_id_type=MESH)
    pl.semaphore_wait(barrier, len(greet))

    for copy in metas + loads:
        copy.wait()
    for s in range(steps):
        for k in range(1, en):
            along(s, k).start()
    sent = []
    for i, peer in enumerate(others):
        sent.append(remote(ids_ref, ids.at[e, d], ms.at[0, i], mr.at[0, i], peer))
        sent.append(remote(probs_ref, probs.at[e, d], ms.at[1, i], mr.at[1, i], peer))
    for copy in sent:
        copy.start()

    for copy in acts:
        copy.wait()

    def prepare(j, carry):
        g = gate[j].astype(f32)
        hid[j] = (g * jax.nn.sigmoid(g) * up[j].astype(f32)).astype(bf16)
        acc[j] = jnp.zeros(acc.shape[1:], f32)
        return carry

    lax.fori_loop(0, local, prepare, 0)

    def pass_on(s):
        for k in range(1, en):
            along(s, k).wait_recv()
            over(s, k).start()
            mate_own(s, k).start()

    pass_on(0)
    far_send(0).start()
    for copy in sent:
        copy.wait_recv()

    spot = lax.broadcasted_iota(jnp.int32, (total, total), 0)
    lane = lax.broadcasted_iota(jnp.int32, (total, total), 1)
    below = ((spot < lane) & (spot // tokens == lane // tokens)).astype(f32).astype(bf16)
    here = e * local + lax.broadcasted_iota(jnp.int32, (local, total), 0)
    origin = (lax.broadcasted_iota(jnp.int32, (local, total), 1) // tokens * cap).astype(f32)
    top = ids.shape[2]

    def find(which, replica):
        named = jnp.zeros((local, total), f32)
        carried = jnp.zeros((local, total), f32)
        id_all = jnp.concatenate([ids[b, replica] for b in range(en)], axis=1)
        pr_all = jnp.concatenate([probs[b, replica].astype(f32) for b in range(en)], axis=1)
        for k in range(top):
            hit = id_all[k : k + 1, :] == here
            named = jnp.where(hit, 1.0, named)
            carried = jnp.where(hit, pr_all[k : k + 1, :], carried)
        position = jnp.dot(named.astype(bf16), below, preferred_element_type=f32)
        code = jnp.where(named > 0.0, position + origin, -1.0)
        match = code[:, None, :] == lax.broadcasted_iota(jnp.int32, (local, slots, total), 1).astype(f32)
        one[which] = jnp.where(match, 1.0, 0.0).reshape(local * slots, total).astype(bf16)
        return jnp.sum(jnp.where(match, carried[:, None, :], 0.0), axis=2, keepdims=True)

    prob[...] = find(0, d)
    find(1, far)
    hs[...] = (prob[...] * hid[...].astype(f32)).astype(bf16)

    def pick(which, src):
        found = jnp.dot(one[which], src, preferred_element_type=f32)
        return found.reshape(local, slots, region).astype(bf16)

    def store_rows(s, p):
        g = index(s, p) - d * steps
        return pltpu.make_async_copy(
            rows.at[s - per, p],
            rows_out.at[:, pl.ds(0, slots), pl.ds(pl.multiple_of(g * region, region), region)],
            lo.at[s - per, p],
        )

    def work(s, r, p, mid):
        weights(r).wait()
        g = index(s, p)
        into = rows.at[lax.rem(s, per), p]
        into[...] = pick(0, tok[g])

        @pl.when(s >= per)
        def _():
            store_rows(s, p).start()

        slot = lax.rem(r, RING)

        def one_expert(j, carry):
            acc[j] += lax.dot_general(
                wbuf[slot, j], into[j], (((1,), (1,)), ((), ())), preferred_element_type=f32
            )
            return carry

        lax.fori_loop(0, local // 2, one_expert, 0, unroll=4)
        mid()
        lax.fori_loop(local // 2, local, one_expert, 0, unroll=4)

        @pl.when(r + RING < 2 * steps)
        def _():
            weights(r + RING).start()

    def step(s, carry):
        for k in range(1, en):
            mate_own(s, k).wait_recv()

        def middle():
            for k in range(1, en):
                over(s, k).wait_recv()
                mate_over(s, k).start()

            @pl.when(s + 1 < steps)
            def _():
                pass_on(s + 1)

            @pl.when(s + 1 < per)
            def _():
                far_send(s + 1).start()

            @pl.when(s + 1 == per)
            def _():
                hid_send().start()

        work(s, 2 * s, plane, middle)
        for k in range(1, en):
            mate_over(s, k).wait_recv()

        def later():
            @pl.when(s >= per)
            def _():
                i = s - per
                far_send(i).wait_recv()
                far_over(i).start()
                far_mate(i).start()

        work(s, 2 * s + 1, 1 - plane, later)
        return carry

    lax.fori_loop(0, steps, step, 0)

    column = lax.broadcasted_iota(jnp.int32, (slots, cells.shape[2]), 1)

    def finish(j, dots):
        grad = acc[j].T
        gh[j] = grad
        dot = jnp.sum(grad * hid[j].astype(f32), axis=1, keepdims=True)
        return jnp.where(column == j, dot, dots)

    dots = lax.fori_loop(0, local, finish, jnp.zeros(column.shape, f32), unroll=4)
    for b in range(en):
        cells[b, pl.ds(0, cap), :] = dots[b * cap : (b + 1) * cap, :]
        cells[b, pl.ds(cap, cells.shape[1] - cap), :] = jnp.zeros((cells.shape[1] - cap, cells.shape[2]), f32)
    for i in range(per):
        far_over(i).wait_recv()
        far_mate_over(i).start()
    returns = [
        remote(cells.at[peer[1]], back.at[t, e], rs.at[i], rr.at[i], peer) for i, peer in enumerate(group)
    ]
    for copy in returns:
        copy.start()
    back[t, e] = cells[e]
    outs = [
        pltpu.make_async_copy(gh, gh_out, lm.at[0]),
        pltpu.make_async_copy(prob, prob_out, lm.at[1]),
        pltpu.make_async_copy(hs, hs_out.at[:, pl.ds(0, slots), :], la.at[0]),
    ]
    for copy in outs:
        copy.start()
    for i in range(per):
        far_mate(i).wait_recv()
        far_mate_over(i).wait_recv()
    far_outs = []
    for q in range(steps):
        far_rows[q] = pick(1, oth[q])
        copy = pltpu.make_async_copy(
            far_rows.at[q], rows_out.at[:, pl.ds(slots, slots), pl.ds(q * region, region)], lx.at[q]
        )
        copy.start()
        far_outs.append(copy)
    hid_send().wait_recv()
    copy = pltpu.make_async_copy(hs_far, hs_out.at[:, pl.ds(slots, slots), :], la.at[1])
    copy.start()
    outs.append(copy)

    def drain(s, carry):
        for k in range(1, en):
            along(s, k).wait_send()
            over(s, k).wait_send()
            mate_own(s, k).wait_send()
            mate_over(s, k).wait_send()
        return carry

    lax.fori_loop(0, steps, drain, 0)
    for copy in sent:
        copy.wait_send()
    hid_send().wait_send()
    for i in range(per):
        far_send(i).wait_send()
        far_over(i).wait_send()
        far_mate(i).wait_send()
        far_mate_over(i).wait_send()
        for p in range(2):
            store_rows(per + i, p).wait()
    for copy in returns:
        copy.wait()
    for copy in outs + far_outs:
        copy.wait()


def expert_kernel(cap, local, rows, hs, gh, gate, up, prob, back, ids, grad_gate, grad_up, grad_w, grad_probs):
    f32, bf16 = jnp.float32, jnp.bfloat16
    for k in range(rows.shape[0]):
        turned = hs[k].astype(f32).T.astype(bf16)
        grad_w[k] = jnp.dot(turned, rows[k], preferred_element_type=f32).astype(bf16)
        g = gate[0, k].astype(f32)
        u = up[0, k].astype(f32)
        s = jax.nn.sigmoid(g)
        weighted = prob[k] * gh[k]
        grad_up[0, k] = (weighted * (g * s)).astype(bf16)
        grad_gate[0, k] = (weighted * u * s * (1.0 + g * (1.0 - s))).astype(bf16)

    @pl.when(pl.program_id(0) == 0)
    def _():
        top, tokens = ids.shape
        tn, en = back.shape[0], back.shape[1]
        summed = back[0]
        for i in range(1, tn):
            summed = summed + back[i]
        cell = jnp.concatenate([summed[b].T[:local] for b in range(en)], axis=0)
        every = lax.broadcasted_iota(jnp.int32, (en * local, tokens), 0)
        spot = lax.broadcasted_iota(jnp.int32, (tokens, tokens), 0)
        lane = lax.broadcasted_iota(jnp.int32, (tokens, tokens), 1)
        below = (spot < lane).astype(f32).astype(bf16)
        named = jnp.zeros(every.shape, f32)
        for k in range(top):
            named = jnp.where(ids[k : k + 1, :] == every, 1.0, named)
        before = jnp.dot(named.astype(bf16), below, preferred_element_type=f32)
        value = jnp.zeros(every.shape, f32)
        for p in range(cap):
            value = jnp.where(before == float(p), cell[:, p : p + 1], value)
        for k in range(top):
            found = jnp.where(ids[k : k + 1, :] == every, value, 0.0)
            grad_probs[k : k + 1, :] = jnp.sum(found, axis=0, keepdims=True)


def on_device(grad_out, route_ids, route_probs, gate_act, up_act, w_down):
    tokens, width = grad_out.shape
    top = route_ids.shape[1]
    tn, en, rn = lax.axis_size("tensor"), lax.axis_size("expert"), lax.axis_size("dp")
    local, units, slots = w_down.shape[0], w_down.shape[1], gate_act.shape[2]
    cap = slots // en
    half = width // rn
    steps = 4
    per = steps // 2
    region = width // (2 * steps)
    total = en * tokens
    f32, bf16 = jnp.float32, jnp.bfloat16
    sem = pltpu.SemaphoreType.DMA
    anyspace = pl.BlockSpec(memory_space=pl.ANY)
    vmem = pl.BlockSpec(memory_space=pltpu.VMEM)
    ids_turned = route_ids.T
    both = rn * slots
    hidden_shape = (local, slots, units)
    rows, hs, gh, prob, back = pl.pallas_call(
        functools.partial(gather_kernel, (tn, en, rn), cap),
        out_shape=(
            jax.ShapeDtypeStruct((local, both, half), bf16),
            jax.ShapeDtypeStruct((local, both, units), bf16),
            jax.ShapeDtypeStruct(hidden_shape, f32),
            jax.ShapeDtypeStruct((local, slots, 1), f32),
            jax.ShapeDtypeStruct((tn, en, 8, 128), f32),
        ),
        in_specs=[anyspace, vmem, vmem, anyspace, anyspace, anyspace],
        out_specs=(anyspace, anyspace, anyspace, anyspace, vmem),
        scratch_shapes=[
            pltpu.VMEM((2 * steps, total, region), bf16),
            pltpu.VMEM((steps, total, region), bf16),
            pltpu.VMEM((en, rn, top, tokens), jnp.int32),
            pltpu.VMEM((en, rn, top, tokens), bf16),
            pltpu.VMEM(hidden_shape, bf16),
            pltpu.VMEM(hidden_shape, bf16),
            pltpu.VMEM((RING, local, units, region), bf16),
            pltpu.VMEM((per, 2, local, slots, region), bf16),
            pltpu.VMEM((steps, local, slots, region), bf16),
            pltpu.VMEM((rn, local * slots, total), bf16),
            pltpu.VMEM((local, units, slots), f32),
            pltpu.VMEM(hidden_shape, f32),
            pltpu.VMEM(hidden_shape, bf16),
            pltpu.VMEM(hidden_shape, bf16),
            pltpu.VMEM(hidden_shape, bf16),
            pltpu.VMEM((local, slots, 1), f32),
            pltpu.VMEM((en, 8, 128), f32),
            sem((2 * steps,)), sem((2,)), sem((2,)), sem((RING,)), sem((per, 2)),
            sem((steps, en - 1)), sem((steps, en - 1)),
            sem((2, en * rn - 1)), sem((2, en * rn - 1)),
            sem((steps, en - 1)), sem((steps, en - 1)),
            sem((steps, en - 1)), sem((steps, en - 1)),
            sem((steps, en - 1)), sem((steps, en - 1)),
            sem((per,)), sem((per,)), sem((per,)), sem((per,)), sem((per,)), sem((per,)), sem((per,)), sem((per,)),
            sem((2,)), sem((tn * en - 1,)), sem((tn * en - 1,)),
        ],
        compiler_params=pltpu.CompilerParams(
            collective_id=0, has_side_effects=True, vmem_limit_bytes=67043328
        ),
    )(grad_out, ids_turned, route_probs.T, gate_act, up_act, w_down)

    batch = 2

    def block(*shape):
        return pl.BlockSpec((batch,) + shape, lambda i: (i,) + (0,) * len(shape))

    act = pl.BlockSpec((1, batch, slots, units), lambda i: (0, i, 0, 0))
    act_shape = jax.ShapeDtypeStruct((1, local, slots, units), bf16)
    grad_gate, grad_up, grad_w, grad_probs = pl.pallas_call(
        functools.partial(expert_kernel, cap, local),
        grid=(local // batch,),
        in_specs=[
            block(both, half), block(both, units), block(slots, units), act, act, block(slots, 1), vmem, vmem,
        ],
        out_specs=(act, act, block(units, half), vmem),
        out_shape=(
            act_shape, act_shape,
            jax.ShapeDtypeStruct((local, units, half), bf16),
            jax.ShapeDtypeStruct((top, tokens), f32),
        ),
    )(rows, hs, gh, gate_act, up_act, prob, back, ids_turned)
    return grad_gate, grad_up, grad_w, grad_probs.T


def solution(mesh):
    sizes = mesh.shape
    small = sizes["tensor"] == 4 and sizes["dp"] == 2 and sizes["expert"] <= 8
    placed = (
        P(("expert", "dp"), None),
        P(("expert", "dp"), None),
        P(("expert", "dp"), None),
        P("dp", "expert", None, "tensor"),
        P("dp", "expert", None, "tensor"),
        P("expert", "tensor", None),
    )
    return jax.shard_map(
        on_device if small else on_device_wide,
        mesh=mesh,
        in_specs=placed,
        out_specs=(
            P("dp", "expert", None, "tensor"),
            P("dp", "expert", None, "tensor"),
            P("expert", "tensor", "dp"),
            P(("expert", "dp"), None),
        ),
        check_vma=False,
    )
```

time: 139 us -> 85.2 us (0.61)
  local copies, waits for them, and re-layouts: 21.2 us -> 0 us
  other arithmetic: 12.3 us -> 0 us
  Pallas kernels: 94.9 us -> 83.8 us
  matrix products: 9.07 us -> 0 us
    pallas_call x3 -> x2, Pallas kernels: 94.9 us -> 83.8 us  [the longest x1 64.2 us: on_device(): pl.pallas_call(functools.partial(gather_kernel, (tn, en, rn), cap), out_s...]
    dot_general x5 -> x0, matrix products: 9.07 us -> none  [the longest x1 5.38 us: on_device(): jnp.dot(pick(one, d).astype(bf16), flat, preferred_element_type=f32)]
    transpose x3 -> x0, local copies, waits for them, and re-layouts: 5.43 us -> none  [the longest x1 3.21 us: on_device(): flat = jnp.transpose(tok, (1, 3, 2, 0, 4)).reshape(en * tokens, width)]
    reshape x6 -> x0, local copies, waits for them, and re-layouts: 5.33 us -> none  [the longest x1 2.78 us: on_device(): flat = jnp.transpose(tok, (1, 3, 2, 0, 4)).reshape(en * tokens, width)]
    concatenate x2 -> x0, other arithmetic: 4.29 us -> none  [the longest x1 3.62 us: on_device(): scaled = jnp.concatenate([near, far], axis=1)]
    convert_element_type x3 -> x0, other arithmetic: 3.89 us -> none  [the longest x1 2.14 us: on_device(): hidden = (g * jax.nn.sigmoid(g) * up_act[0].astype(f32)).astype(bf16)]
    and x4 -> x0, local copies, waits for them, and re-layouts: 3.68 us -> none  [on_device(): spots[:, :, :, :, None, :] & same]
    unnamed x15 -> x0, local copies, waits for them, and re-layouts: 3.21 us -> none
where the time goes in v1:
time: 85.2 us; the launch traced here: 84.5 us
  Pallas kernels  83.8 us (98%)
    pallas_call x1, Pallas kernels, on_device(): pl.pallas_call(functools.partial(gather_kernel, (tn, en, rn), cap), out_s...  64.2 us
    pallas_call x1, Pallas kernels, on_device(): pl.pallas_call(functools.partial(expert_kernel, cap, local), grid=(local...  19.6 us

profile of v1, /device:TPU:0, one launch (start us, length us, event | category | flops | bytes accessed | tf_op | source)
XLA Modules:
  0.0 84.5 jit_solution(13631140469549399404)
XLA Ops:
  0.6 64.2 %shard_map.93 = (bf16[32,48,2048]{2,1,0:T(8,128)(2,1)}, bf16[32,48,192]{2,1,0:T(8,128)(2,1)}, f32[32,24,192]{2,1,0:T(8,128)}, f32[32,24,1]{2,1,0:T(8,128)}, f32[4,4,8,128]{3,2,1,0:T(8,128)}) custom-call(bf16[64,4096]{1,0:T(8,128)(2,1)} %x_ref.1, s32[8,64]{1,0:T(8,128)} %bitcast.3, bf16[8,64]{1,0:T(8,128)(2,1)} %bitcast.5, bf16[1,32,24,192]{3,2,1,0:T(8,128)(2,1)} %gate.1, ...), custom_call_target="tpu_custom_call" | custom-call | tf_op jit(solution)/shard_map/pallas_call | solution.py:475
  64.8 19.6 %shard_map.94 = (bf16[1,32,24,192]{3,2,1,0:T(8,128)(2,1)}, bf16[1,32,24,192]{3,2,1,0:T(8,128)(2,1)}, bf16[32,192,2048]{2,1,0:T(8,128)(2,1)}, f32[8,64]{1,0:T(8,128)}) custom-call(bf16[32,48,2048]{2,1,0:T(8,128)(2,1)} %get-tuple-element.13.rows, bf16[32,48,192]{2,1,0:T(8,128)(2,1)} %get-tuple-element.14.hs, f32[32,24,192]{2,1,0:T(8,128)} %get-tuple-element.15.gh, ...), custom_call_target="tpu_custom_call" | custom-call | tf_op jit(solution)/shard_map/pallas_call | solution.py:525

commit v2 on v1

--- a/solution.py
+++ b/solution.py
@@ -100,8 +100,8 @@
 
 def gather_kernel(
     sizes, cap, x_ref, ids_ref, probs_ref, gate_ref, up_ref, w_ref,
-    rows_out, hs_out, gh_out, prob_out, back,
-    tok, oth, ids, probs, gate, up, wbuf, rows, far_rows, one, acc, gh, hid, hs, hs_far, prob, cells,
+    rows_out, hs_out, gate_out, up_out, back,
+    tok, oth, ids, probs, gate, up, wbuf, rows, far_rows, one, acc, flat, gh, hid, hs, hs_far, grad_gate, grad_up, prob, cells,
     lx, lm, la, lw, lo, zs, zr, ms, mr, ys, yr, as_, ar, bs, br, xs, xr, ps, pr, qs, qr, us, ur, hsem, rs, rr,
 ):
     tn, en, rn = sizes
@@ -173,8 +173,14 @@
     def hid_send():
         return remote(hs, hs_far, hsem.at[0], hsem.at[1], (t, e, far))
 
+    def turn(r):
+        own = (r == 0) | ((lax.rem(r, 2) == 1) & (r < 2 * steps - 1))
+        s = jnp.where(r == 0, 0, jnp.where(own, (r + 1) // 2, jnp.where(r == 2 * steps - 1, steps - 1, r // 2 - 1)))
+        return s, own
+
     def weights(r):
-        g = index(r // 2, jnp.where(lax.rem(r, 2) == 0, plane, 1 - plane))
+        s, own = turn(r)
+        g = index(s, jnp.where(own, plane, 1 - plane))
         slot = lax.rem(r, RING)
         return pltpu.make_async_copy(
             w_ref.at[:, :, pl.ds(pl.multiple_of(g * region, region), region)], wbuf.at[slot], lw.at[slot]
@@ -194,8 +200,6 @@
     acts = [pltpu.make_async_copy(gate_ref.at[0], gate, la.at[0]), pltpu.make_async_copy(up_ref.at[0], up, la.at[1])]
     for copy in metas + loads + acts:
         copy.start()
-    for r in range(RING):
-        weights(r).start()
 
     others = []
     for i in range(en):
@@ -211,19 +215,28 @@
     barrier = pltpu.get_barrier_semaphore()
     for peer in greet:
         pl.semaphore_signal(barrier, inc=1, device_id=peer, device_id_type=MESH)
-    pl.semaphore_wait(barrier, len(greet))
-
     for copy in metas + loads:
         copy.wait()
-    for s in range(steps):
-        for k in range(1, en):
-            along(s, k).start()
+    for r in range(RING):
+        weights(r).start()
+    pl.semaphore_wait(barrier, len(greet))
+
     sent = []
     for i, peer in enumerate(others):
-        sent.append(remote(ids_ref, ids.at[e, d], ms.at[0, i], mr.at[0, i], peer))
-        sent.append(remote(probs_ref, probs.at[e, d], ms.at[1, i], mr.at[1, i], peer))
+        sent.append(remote(ids.at[e, d], ids.at[e, d], ms.at[0, i], mr.at[0, i], peer))
+        sent.append(remote(probs.at[e, d], probs.at[e, d], ms.at[1, i], mr.at[1, i], peer))
     for copy in sent:
         copy.start()
+    def ranked(n):
+        high = en - 1 - n
+        down = jnp.where(high <= e, high - 1, high)
+        return jnp.where(e < en // 2, down, jnp.where(n >= e, n + 1, n))
+
+    def send_own(s):
+        for n in range(en - 1):
+            along(s, lax.rem(ranked(n) - e + en, en)).start()
+
+    send_own(0)
 
     for copy in acts:
         copy.wait()
@@ -231,19 +244,22 @@
     def prepare(j, carry):
         g = gate[j].astype(f32)
         hid[j] = (g * jax.nn.sigmoid(g) * up[j].astype(f32)).astype(bf16)
-        acc[j] = jnp.zeros(acc.shape[1:], f32)
+        acc[j // 2] = jnp.zeros(acc.shape[1:], f32)
+        flat[j // 2] = jnp.zeros(flat.shape[1:], f32)
         return carry
 
     lax.fori_loop(0, local, prepare, 0)
 
-    def pass_on(s):
-        for k in range(1, en):
+    def pass_on(s, first, last):
+        for n in range(first, last):
+            k = lax.rem(e - ranked(en - 2 - n) + en, en)
             along(s, k).wait_recv()
             over(s, k).start()
             mate_own(s, k).start()
 
-    pass_on(0)
-    far_send(0).start()
+    pass_on(0, 0, 1)
+    send_own(1)
+    pass_on(0, 1, en - 2)
     for copy in sent:
         copy.wait_recv()
 
@@ -270,7 +286,9 @@
         return jnp.sum(jnp.where(match, carried[:, None, :], 0.0), axis=2, keepdims=True)
 
     prob[...] = find(0, d)
-    find(1, far)
+    pass_on(0, en - 2, en - 1)
+    send_own(2)
+    far_send(0).start()
     hs[...] = (prob[...] * hid[...].astype(f32)).astype(bf16)
 
     def pick(which, src):
@@ -285,109 +303,159 @@
             lo.at[s - per, p],
         )
 
-    def work(s, r, p, mid):
+    def own_ready(s):
+        for k in range(1, en):
+            mate_own(s, k).wait_recv()
+
+    def over_ready(s):
+        for k in range(1, en):
+            mate_over(s, k).wait_recv()
+
+    def relay(s):
+        for k in range(1, en):
+            over(s, k).wait_recv()
+            mate_over(s, k).start()
+
+    def far_relay(i):
+        far_send(i).wait_recv()
+        far_over(i).start()
+        far_mate(i).start()
+
+    def far_last(i):
+        far_over(i).wait_recv()
+        far_mate_over(i).start()
+
+    def turn_0():
+        own_ready(0)
+
+    def turn_1():
+        send_own(3)
+        pass_on(1, 0, en - 1)
+        far_send(1).start()
+        relay(0)
+        own_ready(1)
+
+    def turn_2():
+        pass_on(2, 0, en - 1)
+        hid_send().start()
+        over_ready(0)
+
+    def turn_3():
+        relay(1)
+        own_ready(2)
+
+    def turn_4():
+        pass_on(3, 0, en - 1)
+        over_ready(1)
+        far_relay(0)
+        far_relay(1)
+
+    def turn_5():
+        relay(2)
+        own_ready(3)
+
+    def turn_6():
+        relay(3)
+        over_ready(2)
+
+    def turn_7():
+        over_ready(3)
+
+    turns = [turn_0, turn_1, turn_2, turn_3, turn_4, turn_5, turn_6, turn_7]
+
+    def step(r, carry):
+        s, own = turn(r)
+        plane_now = jnp.where(own, plane, 1 - plane)
+        slot = lax.rem(r, RING)
+        for n, arrive in enumerate(turns):
+            pl.when(r == n)(arrive)
         weights(r).wait()
-        g = index(s, p)
-        into = rows.at[lax.rem(s, per), p]
-        into[...] = pick(0, tok[g])
+        into = rows.at[lax.rem(s, per), plane_now]
+        into[...] = pick(0, tok[index(s, plane_now)])
 
         @pl.when(s >= per)
         def _():
-            store_rows(s, p).start()
-
-        slot = lax.rem(r, RING)
-
-        def one_expert(j, carry):
-            acc[j] += lax.dot_general(
-                wbuf[slot, j], into[j], (((1,), (1,)), ((), ())), preferred_element_type=f32
+            store_rows(s, plane_now).start()
+
+        def two_experts(i, carry):
+            acc[i] += lax.dot_general(
+                wbuf[slot, 2 * i], into[2 * i], (((1,), (1,)), ((), ())), preferred_element_type=f32
+            )
+            flat[i] += lax.dot_general(
+                into[2 * i + 1], wbuf[slot, 2 * i + 1], (((1,), (1,)), ((), ())), preferred_element_type=f32
             )
             return carry
 
-        lax.fori_loop(0, local // 2, one_expert, 0, unroll=4)
-        mid()
-        lax.fori_loop(local // 2, local, one_expert, 0, unroll=4)
+        lax.fori_loop(0, local // 2, two_experts, 0, unroll=True)
 
         @pl.when(r + RING < 2 * steps)
         def _():
             weights(r + RING).start()
 
-    def step(s, carry):
-        for k in range(1, en):
-            mate_own(s, k).wait_recv()
-
-        def middle():
-            for k in range(1, en):
-                over(s, k).wait_recv()
-                mate_over(s, k).start()
-
-            @pl.when(s + 1 < steps)
-            def _():
-                pass_on(s + 1)
-
-            @pl.when(s + 1 < per)
-            def _():
-                far_send(s + 1).start()
-
-            @pl.when(s + 1 == per)
-            def _():
-                hid_send().start()
-
-        work(s, 2 * s, plane, middle)
-        for k in range(1, en):
-            mate_over(s, k).wait_recv()
-
-        def later():
-            @pl.when(s >= per)
-            def _():
-                i = s - per
-                far_send(i).wait_recv()
-                far_over(i).start()
-                far_mate(i).start()
-
-        work(s, 2 * s + 1, 1 - plane, later)
         return carry
 
-    lax.fori_loop(0, steps, step, 0)
-
+    lax.fori_loop(0, 2 * steps, step, 0)
+
+    far_last(0)
     column = lax.broadcasted_iota(jnp.int32, (slots, cells.shape[2]), 1)
 
-    def finish(j, dots):
-        grad = acc[j].T
-        gh[j] = grad
-        dot = jnp.sum(grad * hid[j].astype(f32), axis=1, keepdims=True)
-        return jnp.where(column == j, dot, dots)
-
-    dots = lax.fori_loop(0, local, finish, jnp.zeros(column.shape, f32), unroll=4)
+    def finish(i, dots):
+        for j, grad in ((2 * i, acc[i].T), (2 * i + 1, flat[i])):
+            gh[j] = grad
+            dot = jnp.sum(grad * hid[j].astype(f32), axis=1, keepdims=True)
+            dots = jnp.where(column == j, dot, dots)
+        return dots
+
+    dots = lax.fori_loop(0, local // 2, finish, jnp.zeros(column.shape, f32), unroll=8)
     for b in range(en):
         cells[b, pl.ds(0, cap), :] = dots[b * cap : (b + 1) * cap, :]
         cells[b, pl.ds(cap, cells.shape[1] - cap), :] = jnp.zeros((cells.shape[1] - cap, cells.shape[2]), f32)
-    for i in range(per):
-        far_over(i).wait_recv()
-        far_mate_over(i).start()
     returns = [
         remote(cells.at[peer[1]], back.at[t, e], rs.at[i], rr.at[i], peer) for i, peer in enumerate(group)
     ]
     for copy in returns:
         copy.start()
-    back[t, e] = cells[e]
+    keep = pltpu.make_async_copy(cells.at[e], back.at[t, e], la.at[0])
+    keep.start()
     outs = [
-        pltpu.make_async_copy(gh, gh_out, lm.at[0]),
-        pltpu.make_async_copy(prob, prob_out, lm.at[1]),
-        pltpu.make_async_copy(hs, hs_out.at[:, pl.ds(0, slots), :], la.at[0]),
+        pltpu.make_async_copy(hs, hs_out.at[:, pl.ds(0, slots), :], lx.at[steps]),
+        pltpu.make_async_copy(grad_gate, gate_out, lm.at[0]),
+        pltpu.make_async_copy(grad_up, up_out, lm.at[1]),
     ]
-    for copy in outs:
+    outs[0].start()
+
+    def activations(j, carry):
+        g = gate[j].astype(f32)
+        u = up[j].astype(f32)
+        s = jax.nn.sigmoid(g)
+        weighted = prob[j] * gh[j]
+        grad_up[j] = (weighted * (g * s)).astype(bf16)
+        grad_gate[j] = (weighted * u * s * (1.0 + g * (1.0 - s))).astype(bf16)
+        return carry
+
+    lax.fori_loop(0, local, activations, 0, unroll=4)
+    find(1, far)
+    for copy in outs[1:]:
         copy.start()
+    far_last(1)
+    far_outs = []
+
+    def far_pick(q):
+        far_rows[q] = pick(1, oth[q])
+        return pltpu.make_async_copy(
+            far_rows.at[q],
+            rows_out.at[:, pl.ds(slots, slots), pl.ds(pl.multiple_of(q * region, region), region)],
+            lx.at[len(far_outs)],
+        )
+
     for i in range(per):
         far_mate(i).wait_recv()
+        far_outs.append(far_pick(plane * per + i))
+        far_outs[-1].start()
+    for i in range(per):
         far_mate_over(i).wait_recv()
-    far_outs = []
-    for q in range(steps):
-        far_rows[q] = pick(1, oth[q])
-        copy = pltpu.make_async_copy(
-            far_rows.at[q], rows_out.at[:, pl.ds(slots, slots), pl.ds(q * region, region)], lx.at[q]
-        )
-        copy.start()
-        far_outs.append(copy)
+        far_outs.append(far_pick((1 - plane) * per + i))
+        far_outs[-1].start()
     hid_send().wait_recv()
     copy = pltpu.make_async_copy(hs_far, hs_out.at[:, pl.ds(slots, slots), :], la.at[1])
     copy.start()
@@ -414,44 +482,105 @@
             store_rows(per + i, p).wait()
     for copy in returns:
         copy.wait()
-    for copy in outs + far_outs:
+    for copy in outs + far_outs + [keep]:
         copy.wait()
 
 
-def expert_kernel(cap, local, rows, hs, gh, gate, up, prob, back, ids, grad_gate, grad_up, grad_w, grad_probs):
+def weight_kernel(
+    cap, chunk, rows_ref, hs_ref, gate_ref, up_ref, back_ref, ids_ref,
+    gate_out, up_out, w_out, probs_out,
+    rows, hs, back, ids, grad_gate, grad_up, grad_w, grad_probs,
+    sm, sr, sh, so, sg,
+):
     f32, bf16 = jnp.float32, jnp.bfloat16
-    for k in range(rows.shape[0]):
-        turned = hs[k].astype(f32).T.astype(bf16)
-        grad_w[k] = jnp.dot(turned, rows[k], preferred_element_type=f32).astype(bf16)
-        g = gate[0, k].astype(f32)
-        u = up[0, k].astype(f32)
-        s = jax.nn.sigmoid(g)
-        weighted = prob[k] * gh[k]
-        grad_up[0, k] = (weighted * (g * s)).astype(bf16)
-        grad_gate[0, k] = (weighted * u * s * (1.0 + g * (1.0 - s))).astype(bf16)
-
-    @pl.when(pl.program_id(0) == 0)
-    def _():
-        top, tokens = ids.shape
-        tn, en = back.shape[0], back.shape[1]
-        summed = back[0]
-        for i in range(1, tn):
-            summed = summed + back[i]
-        cell = jnp.concatenate([summed[b].T[:local] for b in range(en)], axis=0)
-        every = lax.broadcasted_iota(jnp.int32, (en * local, tokens), 0)
-        spot = lax.broadcasted_iota(jnp.int32, (tokens, tokens), 0)
-        lane = lax.broadcasted_iota(jnp.int32, (tokens, tokens), 1)
-        below = (spot < lane).astype(f32).astype(bf16)
-        named = jnp.zeros(every.shape, f32)
-        for k in range(top):
-            named = jnp.where(ids[k : k + 1, :] == every, 1.0, named)
-        before = jnp.dot(named.astype(bf16), below, preferred_element_type=f32)
-        value = jnp.zeros(every.shape, f32)
-        for p in range(cap):
-            value = jnp.where(before == float(p), cell[:, p : p + 1], value)
-        for k in range(top):
-            found = jnp.where(ids[k : k + 1, :] == every, value, 0.0)
-            grad_probs[k : k + 1, :] = jnp.sum(found, axis=0, keepdims=True)
+    local = rows.shape[0]
+    count = local // chunk
+
+    def part(ref, c):
+        return ref.at[pl.ds(c * chunk, chunk)]
+
+    def load(c):
+        return pltpu.make_async_copy(part(rows_ref, c), part(rows, c), sr.at[c])
+
+    def load_hs(c):
+        return pltpu.make_async_copy(part(hs_ref, c), part(hs, c), sh.at[c])
+
+    def store(j):
+        return pltpu.make_async_copy(grad_w.at[j], w_out.at[j], so.at[j])
+
+    small = [(back_ref, back), (ids_ref, ids), (gate_ref, grad_gate), (up_ref, grad_up)]
+    small = [pltpu.make_async_copy(a, b, sm.at[n]) for n, (a, b) in enumerate(small)]
+    small[0].start()
+    small[1].start()
+    load_hs(0).start()
+    load(0).start()
+    small[0].wait()
+    small[1].wait()
+
+    top, tokens = ids.shape
+    tn, en = back.shape[0], back.shape[1]
+    summed = back[0]
+    for i in range(1, tn):
+        summed = summed + back[i]
+    cell = jnp.concatenate([summed[b].T[:local] for b in range(en)], axis=0)
+    every = lax.broadcasted_iota(jnp.int32, (en * local, tokens), 0)
+    spot = lax.broadcasted_iota(jnp.int32, (tokens, tokens), 0)
+    lane = lax.broadcasted_iota(jnp.int32, (tokens, tokens), 1)
+    below = (spot < lane).astype(f32).astype(bf16)
+    named = jnp.zeros(every.shape, f32)
+    for k in range(top):
+        named = jnp.where(ids[k : k + 1, :] == every, 1.0, named)
+    before = jnp.dot(named.astype(bf16), below, preferred_element_type=f32)
+    value = jnp.zeros(every.shape, f32)
+    for p in range(cap):
+        value = jnp.where(before == float(p), cell[:, p : p + 1], value)
+    for k in range(top):
+        found = jnp.where(ids[k : k + 1, :] == every, value, 0.0)
+        grad_probs[k : k + 1, :] = jnp.sum(found, axis=0, keepdims=True)
+    ends = [
+        pltpu.make_async_copy(grad_probs, probs_out, sg.at[0]),
+        pltpu.make_async_copy(grad_gate, gate_out.at[0], sg.at[1]),
+        pltpu.make_async_copy(grad_up, up_out.at[0], sg.at[2]),
+    ]
+    ends[0].start()
+    load_hs(0).wait()
+    load(0).wait()
+    for c in range(1, count):
+        load_hs(c).start()
+        load(c).start()
+    small[2].start()
+    small[3].start()
+
+    def one_chunk(c, carry):
+        @pl.when(c > 0)
+        def _():
+            load_hs(c).wait()
+            load(c).wait()
+
+        @pl.when(c == count - 1)
+        def _():
+            small[2].wait()
+            small[3].wait()
+            ends[1].start()
+            ends[2].start()
+
+        for k in range(chunk):
+            j = c * chunk + k
+            turned = hs[j].astype(f32).T.astype(bf16)
+            grad_w[j] = jnp.dot(turned, rows[j], preferred_element_type=f32).astype(bf16)
+            store(j).start()
+
+        return carry
+
+    lax.fori_loop(0, count, one_chunk, 0)
+
+    def stored(j, carry):
+        store(j).wait()
+        return carry
+
+    lax.fori_loop(0, local, stored, 0)
+    for copy in ends:
+        copy.wait()
 
 
 def on_device(grad_out, route_ids, route_probs, gate_act, up_act, w_down):
@@ -468,21 +597,20 @@
     f32, bf16 = jnp.float32, jnp.bfloat16
     sem = pltpu.SemaphoreType.DMA
     anyspace = pl.BlockSpec(memory_space=pl.ANY)
-    vmem = pl.BlockSpec(memory_space=pltpu.VMEM)
     ids_turned = route_ids.T
     both = rn * slots
     hidden_shape = (local, slots, units)
-    rows, hs, gh, prob, back = pl.pallas_call(
+    rows, hs, early_gate, early_up, back = pl.pallas_call(
         functools.partial(gather_kernel, (tn, en, rn), cap),
         out_shape=(
             jax.ShapeDtypeStruct((local, both, half), bf16),
             jax.ShapeDtypeStruct((local, both, units), bf16),
-            jax.ShapeDtypeStruct(hidden_shape, f32),
-            jax.ShapeDtypeStruct((local, slots, 1), f32),
+            jax.ShapeDtypeStruct(hidden_shape, bf16),
+            jax.ShapeDtypeStruct(hidden_shape, bf16),
             jax.ShapeDtypeStruct((tn, en, 8, 128), f32),
         ),
-        in_specs=[anyspace, vmem, vmem, anyspace, anyspace, anyspace],
-        out_specs=(anyspace, anyspace, anyspace, anyspace, vmem),
+        in_specs=[anyspace] * 6,
+        out_specs=(anyspace,) * 5,
         scratch_shapes=[
             pltpu.VMEM((2 * steps, total, region), bf16),
             pltpu.VMEM((steps, total, region), bf16),
@@ -494,8 +622,11 @@
             pltpu.VMEM((per, 2, local, slots, region), bf16),
             pltpu.VMEM((steps, local, slots, region), bf16),
             pltpu.VMEM((rn, local * slots, total), bf16),
-            pltpu.VMEM((local, units, slots), f32),
+            pltpu.VMEM((local // 2, units, slots), f32),
+            pltpu.VMEM((local // 2, slots, units), f32),
             pltpu.VMEM(hidden_shape, f32),
+            pltpu.VMEM(hidden_shape, bf16),
+            pltpu.VMEM(hidden_shape, bf16),
             pltpu.VMEM(hidden_shape, bf16),
             pltpu.VMEM(hidden_shape, bf16),
             pltpu.VMEM(hidden_shape, bf16),
@@ -515,26 +646,30 @@
         ),
     )(grad_out, ids_turned, route_probs.T, gate_act, up_act, w_down)
 
-    batch = 2
-
-    def block(*shape):
-        return pl.BlockSpec((batch,) + shape, lambda i: (i,) + (0,) * len(shape))
-
-    act = pl.BlockSpec((1, batch, slots, units), lambda i: (0, i, 0, 0))
-    act_shape = jax.ShapeDtypeStruct((1, local, slots, units), bf16)
+    chunk = 8
     grad_gate, grad_up, grad_w, grad_probs = pl.pallas_call(
-        functools.partial(expert_kernel, cap, local),
-        grid=(local // batch,),
-        in_specs=[
-            block(both, half), block(both, units), block(slots, units), act, act, block(slots, 1), vmem, vmem,
-        ],
-        out_specs=(act, act, block(units, half), vmem),
+        functools.partial(weight_kernel, cap, chunk),
+        in_specs=[anyspace] * 6,
+        out_specs=(anyspace,) * 4,
         out_shape=(
-            act_shape, act_shape,
+            jax.ShapeDtypeStruct((1,) + hidden_shape, bf16),
+            jax.ShapeDtypeStruct((1,) + hidden_shape, bf16),
             jax.ShapeDtypeStruct((local, units, half), bf16),
             jax.ShapeDtypeStruct((top, tokens), f32),
         ),
-    )(rows, hs, gh, gate_act, up_act, prob, back, ids_turned)
+        scratch_shapes=[
+            pltpu.VMEM((local, both, half), bf16),
+            pltpu.VMEM((local, both, units), bf16),
+            pltpu.VMEM((tn, en, 8, 128), f32),
+            pltpu.VMEM((top, tokens), jnp.int32),
+            pltpu.VMEM(hidden_shape, bf16),
+            pltpu.VMEM(hidden_shape, bf16),
+            pltpu.VMEM((local, units, half), bf16),
+            pltpu.VMEM((top, tokens), f32),
+            sem((4,)), sem((local // chunk,)), sem((local // chunk,)), sem((local,)), sem((3,)),
+        ],
+        compiler_params=pltpu.CompilerParams(vmem_limit_bytes=67043328),
+    )(rows, hs, early_gate, early_up, back, ids_turned)
     return grad_gate, grad_up, grad_w, grad_probs.T
 
 

time: 85.2 us -> 52.7 us (0.62)
  Pallas kernels: 83.8 us -> 51.9 us
    pallas_call x1, Pallas kernels: 64.2 us -> 39.8 us  [on_device(): pl.pallas_call(functools.partial(gather_kernel, (tn, en, rn), cap), out_s...]
    pallas_call x1, Pallas kernels: 19.6 us -> 12.1 us  [on_device(): pl.pallas_call(functools.partial(weight_kernel, cap, chunk), in_specs=[an...]
where the time goes in v2:
time: 52.7 us; the launch traced here: 52.5 us
  Pallas kernels  51.9 us (98%)
  between operations  0.64 us (1%)
    pallas_call x1, Pallas kernels, on_device(): pl.pallas_call(functools.partial(gather_kernel, (tn, en, rn), cap), out_s...  39.8 us
    pallas_call x1, Pallas kernels, on_device(): pl.pallas_call(functools.partial(weight_kernel, cap, chunk), in_specs=[an...  12.1 us

profile of v2, /device:TPU:0, one launch (start us, length us, event | category | flops | bytes accessed | tf_op | source)
XLA Modules:
  0.0 52.5 jit_solution(17549958245895581228)
XLA Ops:
  0.6 39.8 %shard_map.93 = (bf16[32,48,2048]{2,1,0:T(8,128)(2,1)}, bf16[32,48,192]{2,1,0:T(8,128)(2,1)}, bf16[32,24,192]{2,1,0:T(8,128)(2,1)}, bf16[32,24,192]{2,1,0:T(8,128)(2,1)}, f32[4,4,8,128]{3,2,1,0:T(8,128)}) custom-call(bf16[64,4096]{1,0:T(8,128)(2,1)} %x_ref.1, s32[8,64]{1,0:T(8,128)} %bitcast.3, bf16[8,64]{1,0:T(8,128)(2,1)} %bitcast.5, ...), custom_call_target="tpu_custom_call" | custom-call | tf_op jit(solution)/shard_map/pallas_call | solution.py:603
  40.4 12.1 %shard_map.94 = (bf16[1,32,24,192]{3,2,1,0:T(8,128)(2,1)}, bf16[1,32,24,192]{3,2,1,0:T(8,128)(2,1)}, bf16[32,192,2048]{2,1,0:T(8,128)(2,1)}, f32[8,64]{1,0:T(8,128)}) custom-call(bf16[32,48,2048]{2,1,0:T(8,128)(2,1)} %get-tuple-element.13.rows_ref, bf16[32,48,192]{2,1,0:T(8,128)(2,1)} %get-tuple-element.14.hs_ref, ...), custom_call_target="tpu_custom_call" | custom-call | tf_op jit(solution)/shard_map/pallas_call | solution.py:650

commit v3 on v2

--- a/solution.py
+++ b/solution.py
@@ -102,7 +102,7 @@
     sizes, cap, x_ref, ids_ref, probs_ref, gate_ref, up_ref, w_ref,
     rows_out, hs_out, gate_out, up_out, back,
     tok, oth, ids, probs, gate, up, wbuf, rows, far_rows, one, acc, flat, gh, hid, hs, hs_far, grad_gate, grad_up, prob, cells,
-    lx, lm, la, lw, lo, zs, zr, ms, mr, ys, yr, as_, ar, bs, br, xs, xr, ps, pr, qs, qr, us, ur, hsem, rs, rr,
+    lx, lm, la, lw, lo, zs, zr, ms, mr, ys, yr, as_, ar, bs, br, xs, xr, qs, qr, hsem, rs, rr,
 ):
     tn, en, rn = sizes
     f32, bf16 = jnp.float32, jnp.bfloat16
@@ -153,22 +153,19 @@
         ref = part(tok, index(s, 1 - plane), block(k), core)
         return remote(ref, ref, bs.at[s, k - 1], br.at[s, k - 1], (mate, e, d))
 
-    def far_send(i):
+    def far_send(q, i):
+        p = plane if q == 0 else 1 - plane
         return remote(
-            wide_part(tok, index(i, plane), core), wide_part(oth, plane * per + i, core), xs.at[i], xr.at[i], (t, e, far)
+            wide_part(tok, index(i, p), core), wide_part(oth, p * per + i, core), xs.at[q, i], xr.at[q, i], (t, e, far)
         )
 
-    def far_over(i):
-        ref = wide_part(oth, plane * per + i, core)
-        return remote(ref, ref, ps.at[i], pr.at[i], (across, e, d))
-
-    def far_mate(i):
-        ref = wide_part(oth, plane * per + i, core)
-        return remote(ref, ref, qs.at[i], qr.at[i], (mate, e, d))
-
-    def far_mate_over(i):
-        ref = wide_part(oth, (1 - plane) * per + i, core)
-        return remote(ref, ref, us.at[i], ur.at[i], (mate, e, d))
+    def far_over():
+        ref = wide_part(oth, plane * per + per - 1, core)
+        return remote(ref, ref, xs.at[1, per - 1], xr.at[1, per - 1], (across, e, d))
+
+    def far_mate(q, i):
+        ref = wide_part(oth, (plane if q == 0 else 1 - plane) * per + i, core)
+        return remote(ref, ref, qs.at[q, i], qr.at[q, i], (mate, e, d))
 
     def hid_send():
         return remote(hs, hs_far, hsem.at[0], hsem.at[1], (t, e, far))
@@ -225,8 +222,6 @@
     for i, peer in enumerate(others):
         sent.append(remote(ids.at[e, d], ids.at[e, d], ms.at[0, i], mr.at[0, i], peer))
         sent.append(remote(probs.at[e, d], probs.at[e, d], ms.at[1, i], mr.at[1, i], peer))
-    for copy in sent:
-        copy.start()
     def ranked(n):
         high = en - 1 - n
         down = jnp.where(high <= e, high - 1, high)
@@ -237,6 +232,8 @@
             along(s, lax.rem(ranked(n) - e + en, en)).start()
 
     send_own(0)
+    for copy in sent:
+        copy.start()
 
     for copy in acts:
         copy.wait()
@@ -244,8 +241,9 @@
     def prepare(j, carry):
         g = gate[j].astype(f32)
         hid[j] = (g * jax.nn.sigmoid(g) * up[j].astype(f32)).astype(bf16)
-        acc[j // 2] = jnp.zeros(acc.shape[1:], f32)
-        flat[j // 2] = jnp.zeros(flat.shape[1:], f32)
+        for q in range(2):
+            acc[q, j // 2] = jnp.zeros(acc.shape[2:], f32)
+            flat[q, j // 2] = jnp.zeros(flat.shape[2:], f32)
         return carry
 
     lax.fori_loop(0, local, prepare, 0)
@@ -288,7 +286,7 @@
     prob[...] = find(0, d)
     pass_on(0, en - 2, en - 1)
     send_own(2)
-    far_send(0).start()
+    far_send(0, 0).start()
     hs[...] = (prob[...] * hid[...].astype(f32)).astype(bf16)
 
     def pick(which, src):
@@ -316,14 +314,9 @@
             over(s, k).wait_recv()
             mate_over(s, k).start()
 
-    def far_relay(i):
-        far_send(i).wait_recv()
-        far_over(i).start()
-        far_mate(i).start()
-
-    def far_last(i):
-        far_over(i).wait_recv()
-        far_mate_over(i).start()
+    def far_relay(q, i):
+        far_send(q, i).wait_recv()
+        far_mate(q, i).start()
 
     def turn_0():
         own_ready(0)
@@ -331,8 +324,9 @@
     def turn_1():
         send_own(3)
         pass_on(1, 0, en - 1)
-        far_send(1).start()
+        far_send(0, 1).start()
         relay(0)
+        far_send(1, 0).start()
         own_ready(1)
 
     def turn_2():
@@ -347,12 +341,13 @@
     def turn_4():
         pass_on(3, 0, en - 1)
         over_ready(1)
-        far_relay(0)
-        far_relay(1)
+        far_relay(0, 0)
 
     def turn_5():
         relay(2)
         own_ready(3)
+        far_relay(0, 1)
+        far_over().start()
 
     def turn_6():
         relay(3)
@@ -360,6 +355,7 @@
 
     def turn_7():
         over_ready(3)
+        far_relay(1, 0)
 
     turns = [turn_0, turn_1, turn_2, turn_3, turn_4, turn_5, turn_6, turn_7]
 
@@ -377,13 +373,16 @@
         def _():
             store_rows(s, plane_now).start()
 
+        def product(a, b):
+            return lax.dot_general(a, b, (((1,), (1,)), ((), ())), preferred_element_type=f32)
+
         def two_experts(i, carry):
-            acc[i] += lax.dot_general(
-                wbuf[slot, 2 * i], into[2 * i], (((1,), (1,)), ((), ())), preferred_element_type=f32
-            )
-            flat[i] += lax.dot_general(
-                into[2 * i + 1], wbuf[slot, 2 * i + 1], (((1,), (1,)), ((), ())), preferred_element_type=f32
-            )
+            for q in range(2):
+                cols = slice(q * piece, (q + 1) * piece)
+                acc[q, i] += product(wbuf[slot, 2 * i, :, cols], into[2 * i, :, cols])
+            for q in range(2):
+                cols = slice(q * piece, (q + 1) * piece)
+                flat[q, i] += product(into[2 * i + 1, :, cols], wbuf[slot, 2 * i + 1, :, cols])
             return carry
 
         lax.fori_loop(0, local // 2, two_experts, 0, unroll=True)
@@ -396,11 +395,12 @@
 
     lax.fori_loop(0, 2 * steps, step, 0)
 
-    far_last(0)
+    far_over().wait_recv()
+    far_mate(1, per - 1).start()
     column = lax.broadcasted_iota(jnp.int32, (slots, cells.shape[2]), 1)
 
     def finish(i, dots):
-        for j, grad in ((2 * i, acc[i].T), (2 * i + 1, flat[i])):
+        for j, grad in ((2 * i, (acc[0, i] + acc[1, i]).T), (2 * i + 1, flat[0, i] + flat[1, i])):
             gh[j] = grad
             dot = jnp.sum(grad * hid[j].astype(f32), axis=1, keepdims=True)
             dots = jnp.where(column == j, dot, dots)
@@ -437,24 +437,18 @@
     find(1, far)
     for copy in outs[1:]:
         copy.start()
-    far_last(1)
     far_outs = []
-
-    def far_pick(q):
+    for i in range(steps):
+        far_mate(i // per, i % per).wait_recv()
+        q = (plane if i < per else 1 - plane) * per + i % per
         far_rows[q] = pick(1, oth[q])
-        return pltpu.make_async_copy(
-            far_rows.at[q],
-            rows_out.at[:, pl.ds(slots, slots), pl.ds(pl.multiple_of(q * region, region), region)],
-            lx.at[len(far_outs)],
+        far_outs.append(
+            pltpu.make_async_copy(
+                far_rows.at[q],
+                rows_out.at[:, pl.ds(slots, slots), pl.ds(pl.multiple_of(q * region, region), region)],
+                lx.at[i],
+            )
         )
-
-    for i in range(per):
-        far_mate(i).wait_recv()
-        far_outs.append(far_pick(plane * per + i))
-        far_outs[-1].start()
-    for i in range(per):
-        far_mate_over(i).wait_recv()
-        far_outs.append(far_pick((1 - plane) * per + i))
         far_outs[-1].start()
     hid_send().wait_recv()
     copy = pltpu.make_async_copy(hs_far, hs_out.at[:, pl.ds(slots, slots), :], la.at[1])
@@ -474,11 +468,9 @@
         copy.wait_send()
     hid_send().wait_send()
     for i in range(per):
-        far_send(i).wait_send()
-        far_over(i).wait_send()
-        far_mate(i).wait_send()
-        far_mate_over(i).wait_send()
         for p in range(2):
+            far_send(p, i).wait_send()
+            far_mate(p, i).wait_send()
             store_rows(per + i, p).wait()
     for copy in returns:
         copy.wait()
@@ -510,13 +502,46 @@
 
     small = [(back_ref, back), (ids_ref, ids), (gate_ref, grad_gate), (up_ref, grad_up)]
     small = [pltpu.make_async_copy(a, b, sm.at[n]) for n, (a, b) in enumerate(small)]
-    small[0].start()
-    small[1].start()
     load_hs(0).start()
     load(0).start()
+    ends = [
+        pltpu.make_async_copy(grad_probs, probs_out, sg.at[0]),
+        pltpu.make_async_copy(grad_gate, gate_out.at[0], sg.at[1]),
+        pltpu.make_async_copy(grad_up, up_out.at[0], sg.at[2]),
+    ]
+    load_hs(0).wait()
+    load(0).wait()
+    for c in range(1, count):
+        load_hs(c).start()
+        load(c).start()
+    for copy in small:
+        copy.start()
+
+    def one_chunk(c, carry):
+        @pl.when(c > 0)
+        def _():
+            load_hs(c).wait()
+            load(c).wait()
+
+        @pl.when(c == count - 1)
+        def _():
+            small[2].wait()
+            small[3].wait()
+            ends[1].start()
+            ends[2].start()
+
+        for k in range(chunk):
+            j = c * chunk + k
+            turned = hs[j].astype(f32).T.astype(bf16)
+            grad_w[j] = jnp.dot(turned, rows[j], preferred_element_type=f32).astype(bf16)
+            store(j).start()
+
+        return carry
+
+    lax.fori_loop(0, count, one_chunk, 0)
+
     small[0].wait()
     small[1].wait()
-
     top, tokens = ids.shape
     tn, en = back.shape[0], back.shape[1]
     summed = back[0]
@@ -537,42 +562,7 @@
     for k in range(top):
         found = jnp.where(ids[k : k + 1, :] == every, value, 0.0)
         grad_probs[k : k + 1, :] = jnp.sum(found, axis=0, keepdims=True)
-    ends = [
-        pltpu.make_async_copy(grad_probs, probs_out, sg.at[0]),
-        pltpu.make_async_copy(grad_gate, gate_out.at[0], sg.at[1]),
-        pltpu.make_async_copy(grad_up, up_out.at[0], sg.at[2]),
-    ]
     ends[0].start()
-    load_hs(0).wait()
-    load(0).wait()
-    for c in range(1, count):
-        load_hs(c).start()
-        load(c).start()
-    small[2].start()
-    small[3].start()
-
-    def one_chunk(c, carry):
-        @pl.when(c > 0)
-        def _():
-            load_hs(c).wait()
-            load(c).wait()
-
-        @pl.when(c == count - 1)
-        def _():
-            small[2].wait()
-            small[3].wait()
-            ends[1].start()
-            ends[2].start()
-
-        for k in range(chunk):
-            j = c * chunk + k
-            turned = hs[j].astype(f32).T.astype(bf16)
-            grad_w[j] = jnp.dot(turned, rows[j], preferred_element_type=f32).astype(bf16)
-            store(j).start()
-
-        return carry
-
-    lax.fori_loop(0, count, one_chunk, 0)
 
     def stored(j, carry):
         store(j).wait()
@@ -622,8 +612,8 @@
             pltpu.VMEM((per, 2, local, slots, region), bf16),
             pltpu.VMEM((steps, local, slots, region), bf16),
             pltpu.VMEM((rn, local * slots, total), bf16),
-            pltpu.VMEM((local // 2, units, slots), f32),
-            pltpu.VMEM((local // 2, slots, units), f32),
+            pltpu.VMEM((2, local // 2, units, slots), f32),
+            pltpu.VMEM((2, local // 2, slots, units), f32),
             pltpu.VMEM(hidden_shape, f32),
             pltpu.VMEM(hidden_shape, bf16),
             pltpu.VMEM(hidden_shape, bf16),
@@ -638,7 +628,7 @@
             sem((steps, en - 1)), sem((steps, en - 1)),
             sem((steps, en - 1)), sem((steps, en - 1)),
             sem((steps, en - 1)), sem((steps, en - 1)),
-            sem((per,)), sem((per,)), sem((per,)), sem((per,)), sem((per,)), sem((per,)), sem((per,)), sem((per,)),
+            sem((2, per)), sem((2, per)), sem((2, per)), sem((2, per)),
             sem((2,)), sem((tn * en - 1,)), sem((tn * en - 1,)),
         ],
         compiler_params=pltpu.CompilerParams(

time: 52.7 us -> 49 us (0.930)
  Pallas kernels: 51.9 us -> 48.2 us
    pallas_call x1, Pallas kernels: 39.8 us -> 36.1 us  [on_device(): pl.pallas_call(functools.partial(gather_kernel, (tn, en, rn), cap), out_s...]
where the time goes in v3:
time: 49 us; the launch traced here: 48.8 us
  Pallas kernels  48.2 us (98%)
  between operations  0.64 us (1%)
    pallas_call x1, Pallas kernels, on_device(): pl.pallas_call(functools.partial(gather_kernel, (tn, en, rn), cap), out_s...  36.1 us
    pallas_call x1, Pallas kernels, on_device(): pl.pallas_call(functools.partial(weight_kernel, cap, chunk), in_specs=[an...  12.1 us

profile of v3, /device:TPU:0, one launch (start us, length us, event | category | flops | bytes accessed | tf_op | source)
XLA Modules:
  0.0 48.8 jit_solution(10802618797305406828)
XLA Ops:
  0.6 36.1 %shard_map.93 = (bf16[32,48,2048]{2,1,0:T(8,128)(2,1)}, bf16[32,48,192]{2,1,0:T(8,128)(2,1)}, bf16[32,24,192]{2,1,0:T(8,128)(2,1)}, bf16[32,24,192]{2,1,0:T(8,128)(2,1)}, f32[4,4,8,128]{3,2,1,0:T(8,128)}) custom-call(bf16[64,4096]{1,0:T(8,128)(2,1)} %x_ref.1, s32[8,64]{1,0:T(8,128)} %bitcast.3, bf16[8,64]{1,0:T(8,128)(2,1)} %bitcast.5, ...), custom_call_target="tpu_custom_call" | custom-call | tf_op jit(solution)/shard_map/pallas_call | solution.py:593
  36.7 12.1 %shard_map.94 = (bf16[1,32,24,192]{3,2,1,0:T(8,128)(2,1)}, bf16[1,32,24,192]{3,2,1,0:T(8,128)(2,1)}, bf16[32,192,2048]{2,1,0:T(8,128)(2,1)}, f32[8,64]{1,0:T(8,128)}) custom-call(bf16[32,48,2048]{2,1,0:T(8,128)(2,1)} %get-tuple-element.13.rows_ref, bf16[32,48,192]{2,1,0:T(8,128)(2,1)} %get-tuple-element.14.hs_ref, ...), custom_call_target="tpu_custom_call" | custom-call | tf_op jit(solution)/shard_map/pallas_call | solution.py:640

commit v4 on v3

--- a/solution.py
+++ b/solution.py
@@ -406,7 +406,7 @@
             dots = jnp.where(column == j, dot, dots)
         return dots
 
-    dots = lax.fori_loop(0, local // 2, finish, jnp.zeros(column.shape, f32), unroll=8)
+    dots = lax.fori_loop(0, local // 2, finish, jnp.zeros(column.shape, f32), unroll=True)
     for b in range(en):
         cells[b, pl.ds(0, cap), :] = dots[b * cap : (b + 1) * cap, :]
         cells[b, pl.ds(cap, cells.shape[1] - cap), :] = jnp.zeros((cells.shape[1] - cap, cells.shape[2]), f32)

time: 49 us -> 48.8 us (level)
  no operation moved by 1% of the time
where the time goes in v4:
time: 48.8 us; the launch traced here: 48.6 us
  Pallas kernels  48 us (98%)
  between operations  0.64 us (1%)
    pallas_call x1, Pallas kernels, on_device(): pl.pallas_call(functools.partial(gather_kernel, (tn, en, rn), cap), out_s...  35.9 us
    pallas_call x1, Pallas kernels, on_device(): pl.pallas_call(functools.partial(weight_kernel, cap, chunk), in_specs=[an...  12.1 us

profile of v4, /device:TPU:0, one launch (start us, length us, event | category | flops | bytes accessed | tf_op | source)
XLA Modules:
  0.0 48.6 jit_solution(16032696186970802744)
XLA Ops:
  0.6 35.9 %shard_map.93 = (bf16[32,48,2048]{2,1,0:T(8,128)(2,1)}, bf16[32,48,192]{2,1,0:T(8,128)(2,1)}, bf16[32,24,192]{2,1,0:T(8,128)(2,1)}, bf16[32,24,192]{2,1,0:T(8,128)(2,1)}, f32[4,4,8,128]{3,2,1,0:T(8,128)}) custom-call(bf16[64,4096]{1,0:T(8,128)(2,1)} %x_ref.1, s32[8,64]{1,0:T(8,128)} %bitcast.3, bf16[8,64]{1,0:T(8,128)(2,1)} %bitcast.5, ...), custom_call_target="tpu_custom_call" | custom-call | tf_op jit(solution)/shard_map/pallas_call | solution.py:593
  36.5 12.1 %shard_map.94 = (bf16[1,32,24,192]{3,2,1,0:T(8,128)(2,1)}, bf16[1,32,24,192]{3,2,1,0:T(8,128)(2,1)}, bf16[32,192,2048]{2,1,0:T(8,128)(2,1)}, f32[8,64]{1,0:T(8,128)}) custom-call(bf16[32,48,2048]{2,1,0:T(8,128)(2,1)} %get-tuple-element.13.rows_ref, bf16[32,48,192]{2,1,0:T(8,128)(2,1)} %get-tuple-element.14.hs_ref, ...), custom_call_target="tpu_custom_call" | custom-call | tf_op jit(solution)/shard_map/pallas_call | solution.py:640
